TPU v7x, 32 devices: a whole 2x2x4 slice. The times are simulated.
32 devices in a mesh: dev: 32 (over z, y, x, core).
Axes of the slice: x: 2, y: 2, z: 4, core: 2. Of those that a mesh axis runs over, the one named last changes fastest.
Arguments:
- occurrence: bfloat16 [2048, 128, 128], P('dev'), may hold values from -0.5 to 0.5
- block_owner: int32 [2048, 1], P('dev'), may hold values from 0 to 31; in each aligned block of 64 rows (0 to 63, 64 to 127, ...) at most 4 rows name the same one
- read_block: int32 [2048], P('dev'), may hold values from 0 to 15
- slot_order: int32 [32, 128], P('dev'), may hold values from 0 to 127, each once within a row
Outputs:
- margin: float32 [65536, 512], P('dev')
Inputs may be any that keep to these rules, and one draw needn't show every extreme that they name: `block_owner`: among the blocks of one device no owner is named more than 4 times, a bound that some block reaches. `slot_order`: each row names every number of 0 to 127 once.
All inputs are finite; a program needn't handle non-finite values.
Results may differ from a plain program's by a relative error of at most 0.0026.
Values may be sent and summed in bfloat16 or wider, within the bound.
A program may use at most 128 MiB of HBM per device.

v0:
```python
import jax
import jax.numpy as jnp
import numpy as np
from jax import lax
from jax.sharding import PartitionSpec as P

CAP = 4
RB_DEV = 16


def shards(occurrence, block_owner, read_block, slot_order):
    devices = lax.axis_size("dev")
    blocks, rows, kmers = occurrence.shape
    per_pair = 2 * blocks // devices
    slot_total = devices * per_pair
    owners = block_owner[:, 0]
    positions = jnp.arange(blocks, dtype=jnp.int32)
    earlier = positions[None, :] < positions[:, None]
    same_owner = owners[:, None] == owners[None, :]
    earlier_count = jnp.sum((same_owner & earlier).astype(jnp.int32), axis=1)
    send_slot = owners * per_pair + earlier_count
    onehot = (send_slot[:, None] == jnp.arange(slot_total, dtype=jnp.int32)[None, :]).astype(
        jnp.bfloat16
    )
    outgoing = jnp.einsum(
        "bs,bik->sik", onehot, occurrence, preferred_element_type=jnp.float32
    ).astype(jnp.bfloat16)
    received = lax.all_to_all(outgoing, "dev", split_axis=0, concat_axis=0, tiled=True)
    order_row = slot_order[0]
    place_of = (
        jnp.zeros((slot_total,), jnp.int32)
        .at[order_row]
        .set(jnp.arange(slot_total, dtype=jnp.int32))
    )
    groups = received[order_row].reshape(slot_total // CAP, CAP, rows, kmers)
    read_onehot = (read_block[None, :] == jnp.arange(RB_DEV, dtype=jnp.int32)[:, None]).astype(
        jnp.bfloat16
    )
    others_table = np.array(
        [[column for column in range(CAP) if column != spot] for spot in range(CAP)], dtype=np.int32
    )
    ordered_partners = groups[:, others_table].reshape(slot_total, CAP - 1, rows, kmers)
    partners = ordered_partners[place_of]
    spot_send = (place_of % CAP).astype(jnp.bfloat16)[:, None]
    returned, spot_back = (
        lax.all_to_all(partners, "dev", split_axis=0, concat_axis=0, tiled=True),
        lax.all_to_all(spot_send, "dev", split_axis=0, concat_axis=0, tiled=True),
    )
    partner_blocks = jnp.einsum(
        "bs,sjrk->bjrk", onehot, returned, preferred_element_type=jnp.float32
    ).astype(jnp.bfloat16)
    spot_value = jnp.dot(onehot, spot_back, preferred_element_type=jnp.float32)[:, 0]
    spot_index = (spot_value + 0.5).astype(jnp.int32)
    stacked = []
    for column in range(CAP):
        below_pick = partner_blocks[:, min(column, CAP - 2)]
        above_pick = partner_blocks[:, max(column - 1, 0)]
        chosen = jnp.where(
            (spot_index == column)[:, None, None],
            occurrence,
            jnp.where((spot_index > column)[:, None, None], below_pick, above_pick),
        )
        stacked.append(chosen)
    partner_full = jnp.stack(stacked, axis=1)
    tile_block = jnp.einsum(
        "bik,bjrk->bijr", occurrence, partner_full, preferred_element_type=jnp.float32
    )
    tile_block = tile_block.astype(jnp.bfloat16).reshape(blocks, rows, CAP * rows)
    summed = jnp.einsum("nb,bic->nic", read_onehot, tile_block, preferred_element_type=jnp.float32)
    return summed.reshape(RB_DEV * rows, CAP * rows)


def solution(mesh):
    placed = (P("dev", None, None), P("dev", None), P("dev"), P("dev", None))
    return jax.shard_map(
        shards, mesh=mesh, in_specs=placed, out_specs=P("dev", None), check_vma=False
    )
```

profile of v0, /device:TPU:0, one launch (start us, length us, event | category | flops | bytes accessed | tf_op | source)
XLA Modules:
  0.0 498.7 jit_solution(5830578073506694928)
XLA Ops:
  0.0 0.9 convert_reduce_fusion
  0.9 0.7 fusion.29
  1.6 3.6 convolution_convert_fusion
  5.2 4.7 copy.41
  9.9 0.0 copy-start.3
  9.9 7.4 %all-to-all-start.1 = ((bf16[128,128,128]{2,1,0:T(8,128)(2,1)}), bf16[128,128,128]{2,1,0:T(8,128)(2,1)}, u32[]{:S(2)}, u32[]{:S(2)}) async-start(bf16[128,128,128]{2,1,0:T(8,128)(2,1)} %copy.41), calls=%async_computation.1 | async-start | bytes 8388608 | tf_op jit(solution)/shard_map/all_to_all | solution.py:28
  17.4 0.0 copy-done.3
  17.4 1.0 scatter_custom_fusion
  18.4 0.7 all_to_all.16
  19.1 91.9 %all-to-all-done.1 = bf16[128,128,128]{2,1,0:T(8,128)(2,1)} async-done(((bf16[128,128,128]{2,1,0:T(8,128)(2,1)}), bf16[128,128,128]{2,1,0:T(8,128)(2,1)}, u32[]{:S(2)}, u32[]{:S(2)}) %all-to-all-start.1) | async-done | bytes 4194336 | tf_op jit(solution)/shard_map/all_to_all | solution.py:28
  111.1 4.1 all-to-all-start
  115.2 0.0 copy-done.2
  115.2 5.3 %gather_fusion = bf16[128,128,128]{2,1,0:T(8,128)(2,1)} fusion(bf16[128,128,128]{2,1,0:T(8,128)(2,1)} %all-to-all-done.1, s32[1024]{0:T(1024)S(1)} %pad_clamp_fusion.2), kind=kCustom, calls=%fused_computation | custom fusion | bytes 8389120 | tf_op jit(solution)/shard_map/gather | solution.py:35
  120.5 4.7 copy.42
  125.2 8.2 %gather_fusion.1 = bf16[12,32,128,128]{3,2,1,0:T(8,128)(2,1)} fusion(bf16[32,4,128,128]{3,2,0,1:T(8,128)(2,1)} %copy.42, s32[1024]{0:T(1024)S(1)} %pad_clamp_fusion.1), kind=kCustom, calls=%fused_computation.1 | custom fusion | bytes 25165872 | tf_op jit(solution)/shard_map/gather | solution.py:42
  133.4 11.8 %copy.43 = bf16[32,4,3,128,128]{4,3,2,1,0:T(8,128)(2,1)} copy(bf16[32,4,3,128,128]{4,3,0,2,1:T(8,128)(2,1)} %bitcast.71) | data formatting | bytes 25165824 | tf_op jit(solution)/shard_map/gather | solution.py:42
  145.2 13.0 %gather_fusion.2 = bf16[128,3,128,128]{3,2,1,0:T(8,128)(2,1)} fusion(bf16[128,3,128,128]{3,2,1,0:T(8,128)(2,1)} %bitcast.72, s32[1024]{0:T(1024)S(1)} %pad_clamp_fusion), kind=kCustom, calls=%fused_computation.2 | custom fusion | bytes 25166336 | tf_op jit(solution)/shard_map/gather | solution.py:43
  158.2 0.0 all-to-all-done
  158.2 6.1 %all-to-all-start.2 = ((bf16[128,3,128,128]{3,2,1,0:T(8,128)(2,1)}), bf16[128,3,128,128]{3,2,1,0:T(8,128)(2,1)}, u32[]{:S(2)}, u32[]{:S(2)}) async-start(bf16[128,3,128,128]{3,2,1,0:T(8,128)(2,1)} %gather_fusion.2), calls=%async_computation.2 | async-start | bytes 25165824 | tf_op jit(solution)/shard_map/all_to_all | solution.py:46
  164.3 0.1 reduce
  164.4 0.1 reshape.111
  164.5 0.2 broadcast_compare_fusion.5
  164.7 278.0 %all-to-all-done.2 = bf16[128,3,128,128]{3,2,1,0:T(8,128)(2,1)} async-done(((bf16[128,3,128,128]{3,2,1,0:T(8,128)(2,1)}), bf16[128,3,128,128]{3,2,1,0:T(8,128)(2,1)}, u32[]{:S(2)}, u32[]{:S(2)}) %all-to-all-start.2) | async-done | bytes 12582944 | tf_op jit(solution)/shard_map/all_to_all | solution.py:46
  442.7 13.4 %fusion.7 = bf16[64,3,128,128]{3,0,2,1:T(8,128)(2,1)S(1)} fusion(bf16[128,3,128,128]{3,2,1,0:T(8,128)(2,1)} %all-to-all-done.2, s32[64]{0:T(128)S(1)} %fusion.29), kind=kOutput, calls=%fused_computation.10 | convolution fusion | flops 808460288 | bytes 18874624 | tf_op jit(solution)/shard_map/bs,sjrk->bjrk/dot_general | solution.py:49
  456.2 0.0 copy-done
  456.2 2.2 select_bitcast_fusion.3
  458.4 3.8 pad_maximum_fusion
  462.2 15.1 %fusion.4 = bf16[64,4,128,128]{3,2,1,0:T(8,128)(2,1)} fusion(bf16[64,4,128,128]{3,0,2,1:T(8,128)(2,1)} %pad_maximum_fusion, bf16[64,128,128]{2,1,0:T(8,128)(2,1)S(1)} %copy-done), kind=kOutput, calls=%fused_computation.9 | convolution fusion | flops 1077936128 | bytes 18874368 | tf_op jit(solution)/shard_map/bik,bjrk->bijr/dot_general | solution.py:65
  477.3 12.3 %copy.50 = bf16[64,128,512]{2,0,1:T(8,128)(2,1)} copy(bf16[64,128,512]{1,2,0:T(8,128)(2,1)} %bitcast.73) | data formatting | bytes 16777216 | tf_op jit(solution)/shard_map/reshape | solution.py:68
  489.6 0.0 copy-done.1
  489.6 4.6 fusion.23
  494.2 4.4 copy.51
  (9 shorter events, 0.0 us)
Async XLA Ops:
  9.9 7.5 %copy-start.3 = (s32[1,128]{1,0:T(1,128)S(1)}, s32[1,128]{1,0:T(1,128)}, u32[]{:S(2)}) copy-start(s32[1,128]{1,0:T(1,128)} %param.9) | copy-start | bytes 1540
  9.9 105.3 %copy-start.2 = (s32[12]{0:T(128)S(1)}, s32[12]{0:T(128)}, u32[]{:S(2)}) copy-start(s32[12]{0:T(128)} %constant.37) | copy-start | bytes 148
  9.9 101.1 %all-to-all-start.1 = ((bf16[128,128,128]{2,1,0:T(8,128)(2,1)}), bf16[128,128,128]{2,1,0:T(8,128)(2,1)}, u32[]{:S(2)}, u32[]{:S(2)}) async-start(bf16[128,128,128]{2,1,0:T(8,128)(2,1)} %copy.41), calls=%async_computation.1 | async-start | bytes 8388608 | tf_op jit(solution)/shard_map/all_to_all | solution.py:28
  111.1 47.2 %all-to-all-start = ((bf16[32,4,1]{1,2,0:T(2,128)(2,1)}), bf16[32,4,1]{1,2,0:T(2,128)(2,1)S(1)}, u32[]{:S(2)}, u32[]{:S(2)}) async-start(bf16[32,4,1]{1,2,0:T(2,128)(2,1)} %all_to_all.16), calls=%async_computation | async-start | bytes 32768 | tf_op jit(solution)/shard_map/all_to_all | solution.py:47
  158.2 284.5 %all-to-all-start.2 = ((bf16[128,3,128,128]{3,2,1,0:T(8,128)(2,1)}), bf16[128,3,128,128]{3,2,1,0:T(8,128)(2,1)}, u32[]{:S(2)}, u32[]{:S(2)}) async-start(bf16[128,3,128,128]{3,2,1,0:T(8,128)(2,1)} %gather_fusion.2), calls=%async_computation.2 | async-start | bytes 25165824 | tf_op jit(solution)/shard_map/all_to_all | solution.py:46
  164.7 291.4 %copy-start = (bf16[64,128,128]{2,1,0:T(8,128)(2,1)S(1)}, bf16[64,128,128]{2,1,0:T(8,128)(2,1)}, u32[]{:S(2)}) copy-start(bf16[64,128,128]{2,1,0:T(8,128)(2,1)} %param.6) | copy-start | bytes 6291460
  477.3 12.3 %copy-start.1 = (s32[64]{0:T(128)S(1)}, s32[64]{0:T(128)}, u32[]{:S(2)}) copy-start(s32[64]{0:T(128)} %param.8) | copy-start | bytes 772
where the time goes:
time: 500 us; the launch traced here: 499 us
  waiting for transfers between devices  370 us (74%)
  local copies, waits for them, and re-layouts  66.3 us (13%)
  matrix products  36.9 us (7%)
  starting transfers between devices  17.7 us (4%)
  other arithmetic  7.73 us (2%)
    all_to_all x1, waiting for transfers between devices, shards(): lax.all_to_all(partners, 'dev', split_axis=0, concat_axis=0, tiled=True)  278 us
    all_to_all x1, waiting for transfers between devices, shards(): lax.all_to_all(outgoing, 'dev', split_axis=0, concat_axis=0, tiled=True)  91.9 us
    gather x2, local copies, waits for them, and re-layouts, shards(): groups[:, others_table].reshape(slot_total, CAP - 1, rows, kmers)  20 us
    dot_general x1, matrix products, shards(): jnp.einsum('bik,bjrk->bijr', occurrence, partner_full, preferred_element_...  15.1 us
    dot_general x1, matrix products, shards(): jnp.einsum('bs,sjrk->bjrk', onehot, returned, preferred_element_type=jnp....  13.4 us
    gather x1, local copies, waits for them, and re-layouts, shards(): partners = ordered_partners[place_of]  13 us
    reshape x1, local copies, waits for them, and re-layouts, shards(): tile_block.astype(jnp.bfloat16).reshape(blocks, rows, CAP * rows)  12.3 us
  transfers between devices with their start and end apart: 3, of which 2 were waited for; matrix products, arithmetic and copies ran while one was open for 9% of the time, Pallas kernels for 0%

commit v1 on v0

--- a/solution.py
+++ b/solution.py
@@ -1,14 +1,18 @@
+import functools
 import jax
 import jax.numpy as jnp
 import numpy as np
 from jax import lax
+from jax.experimental import pallas as pl
+from jax.experimental.pallas import tpu as pltpu
 from jax.sharding import PartitionSpec as P
 
 CAP = 4
 RB_DEV = 16
-
-
-def shards(occurrence, block_owner, read_block, slot_order):
+CORES = 2
+
+
+def exchange_by_owner(occurrence, block_owner, read_block, slot_order):
     devices = lax.axis_size("dev")
     blocks, rows, kmers = occurrence.shape
     per_pair = 2 * blocks // devices
@@ -70,6 +74,187 @@
     return summed.reshape(RB_DEV * rows, CAP * rows)
 
 
+def i32(x):
+    return x.astype(jnp.int32)
+
+
+def iota(*shape, axis):
+    return lax.broadcasted_iota(jnp.int32, shape, axis)
+
+
+def group_table(block_owner, slot_order):
+    devices = lax.axis_size("dev")
+    blocks = block_owner.shape[0]
+    slots = slot_order.shape[1]
+    per_pair = slots // devices
+    mine = jnp.concatenate([block_owner[:, 0], slot_order[0]])
+    everyone = lax.all_gather(mine, "dev", axis=0)
+    owners, order = everyone[:, :blocks], everyone[:, blocks:]
+    earlier = iota(blocks, blocks, axis=1) < iota(blocks, blocks, axis=0)
+    same = owners[:, :, None] == owners[:, None, :]
+    rank = jnp.sum(i32(same & earlier[None]), axis=2)
+    key = owners * per_pair + rank
+    number = iota(devices, blocks, axis=0) * blocks + iota(devices, blocks, axis=1) + 1
+    hit = key[:, :, None] == iota(1, 1, slots, axis=2)
+    holder = jnp.sum(jnp.where(hit, number[:, :, None], 0), axis=1)
+    holder = holder.reshape(devices, devices, per_pair).transpose(1, 0, 2).reshape(devices, slots)
+    turned = order.reshape(devices, slots // CAP, CAP).transpose(2, 0, 1)
+    hit = turned[:, :, :, None] == iota(1, 1, 1, slots, axis=3)
+    table = jnp.sum(jnp.where(hit, holder[None, :, None, :], 0), axis=3)
+    return table.reshape(CAP, devices * slots // CAP)
+
+
+def fullest_lane(table, blocks):
+    devices = lax.axis_size("dev")
+    source = jnp.where(table > 0, (table - 1) // blocks, -1)
+    named = source[:, :, None] == iota(1, 1, devices, axis=2)
+    held = jnp.sum(i32(named), axis=0)
+    held_chip = jnp.sum(held.reshape(-1, devices // CORES, CORES), axis=2)
+    demand = jnp.einsum(
+        "gc,gd->cd",
+        held_chip.astype(jnp.bfloat16),
+        (held > 0).astype(jnp.bfloat16),
+        preferred_element_type=jnp.float32,
+    )
+    chips = devices // CORES
+    away = iota(chips, devices, axis=0) != iota(chips, devices, axis=1) // CORES
+    return jnp.max(jnp.where(away, demand, 0.0))
+
+
+def routes(table, blocks, lane):
+    devices = lax.axis_size("dev")
+    chips = devices // CORES
+    pair = CORES * blocks
+    me = lax.axis_index("dev")
+    chip, core = me // CORES, me % CORES
+    ids = chip * pair + iota(pair, 1, axis=0) + 1
+    inside = (table[0][None] == ids) | (table[1][None] == ids)
+    for j in range(2, CAP):
+        inside = inside | (table[j][None] == ids)
+    partners = jnp.stack(
+        [jnp.sum(jnp.where(inside, table[j][None], 0), axis=1) for j in range(CAP)]
+    )
+    source = jnp.where(partners > 0, (partners - 1) // blocks, -1)
+    named = source[:, :, None] == iota(1, 1, devices, axis=2)
+    need = jnp.any(named, axis=0) & (iota(1, devices, axis=1) // CORES != chip)
+    before = (iota(pair, pair, axis=1) < iota(pair, pair, axis=0)).astype(jnp.bfloat16)
+    rank = i32(jnp.dot(before, need.astype(jnp.bfloat16), preferred_element_type=jnp.float32))
+    rank = jnp.where(need, rank, -1).T
+    x = jnp.arange(pair, dtype=jnp.int32)
+    local = jnp.where(x // blocks == core, x % blocks, blocks + x % blocks)
+    turn = iota(1, lane, 1, axis=1) * CORES + core
+    send = jnp.sum(jnp.where(rank[:, None, :] == turn, local[None, None, :], 0), axis=2)
+
+    own = lax.dynamic_slice(partners, (0, core * blocks), (CAP, blocks)).reshape(-1)
+    total = devices * blocks
+    match = own[:, None] == iota(1, total, axis=1) + 1
+    wanted = jnp.any(match, axis=0).reshape(chips, pair)
+    arrived = i32(
+        jnp.dot(wanted.astype(jnp.bfloat16), before.T, preferred_element_type=jnp.float32)
+    )
+    c = iota(chips, pair, axis=0)
+    there = pair + (c * CORES + arrived % CORES) * lane + arrived // CORES
+    place = jnp.where(c == chip, local[None, :], there).reshape(1, total)
+    empty = pair + devices * lane
+    pick = jnp.sum(jnp.where(match, place, 0), axis=1)
+    pick = jnp.where(own > 0, pick, empty)
+    return send.reshape(-1), pick
+
+
+def pack_kernel(send_ref, own_ref, sib_ref, out_ref, held, sems):
+    blocks = own_ref.shape[0]
+    first = pltpu.make_async_copy(own_ref, held.at[pl.ds(0, blocks)], sems.at[0])
+    second = pltpu.make_async_copy(sib_ref, held.at[pl.ds(blocks, blocks)], sems.at[1])
+    first.start()
+    second.start()
+    first.wait()
+    second.wait()
+
+    def step(i, _):
+        out_ref[i] = held[send_ref[i]]
+        return 0
+
+    lax.fori_loop(0, out_ref.shape[0], step, 0, unroll=4)
+
+
+def tile_kernel(pick_ref, read_ref, own_ref, sib_ref, got_ref, out_ref, held, sems):
+    blocks = own_ref.shape[0]
+    rows = own_ref.shape[1]
+    many = got_ref.shape[0]
+    copies = [
+        pltpu.make_async_copy(own_ref, held.at[pl.ds(0, blocks)], sems.at[0]),
+        pltpu.make_async_copy(sib_ref, held.at[pl.ds(blocks, blocks)], sems.at[1]),
+        pltpu.make_async_copy(got_ref, held.at[pl.ds(2 * blocks, many)], sems.at[2]),
+    ]
+    for copy in copies:
+        copy.start()
+    held[2 * blocks + many] = jnp.zeros(held.shape[1:], held.dtype)
+    out_ref[...] = jnp.zeros_like(out_ref)
+    for copy in copies:
+        copy.wait()
+
+    def step(b, _):
+        others = jnp.concatenate([held[pick_ref[j * blocks + b]] for j in range(CAP)], axis=0)
+        tile = lax.dot_general(
+            held[b], others, (((1,), (1,)), ((), ())), preferred_element_type=jnp.float32
+        )
+        where = pl.ds(pl.multiple_of(read_ref[b] * rows, rows), rows)
+        out_ref[where, :] += tile.astype(jnp.bfloat16).astype(jnp.float32)
+        return 0
+
+    lax.fori_loop(0, blocks, step, 0, unroll=2)
+
+
+def direct(occurrence, sibling, read_block, table, lane):
+    devices = lax.axis_size("dev")
+    blocks, rows, kmers = occurrence.shape
+    many = devices * lane
+    send, pick = routes(table, blocks, lane)
+    smem = pl.BlockSpec(memory_space=pltpu.SMEM)
+    hbm = pl.BlockSpec(memory_space=pl.ANY)
+    vmem = pl.BlockSpec(memory_space=pltpu.VMEM)
+    outgoing = pl.pallas_call(
+        pack_kernel,
+        out_shape=jax.ShapeDtypeStruct((many, rows, kmers), occurrence.dtype),
+        in_specs=[smem, hbm, hbm],
+        out_specs=vmem,
+        scratch_shapes=[
+            pltpu.VMEM((CORES * blocks, rows, kmers), occurrence.dtype),
+            pltpu.SemaphoreType.DMA((2,)),
+        ],
+        compiler_params=pltpu.CompilerParams(vmem_limit_bytes=60 << 20),
+        name="pack",
+    )(send, occurrence, sibling)
+    incoming = lax.all_to_all(outgoing, "dev", split_axis=0, concat_axis=0, tiled=True)
+    return pl.pallas_call(
+        tile_kernel,
+        out_shape=jax.ShapeDtypeStruct((RB_DEV * rows, CAP * rows), jnp.float32),
+        in_specs=[smem, smem, hbm, hbm, hbm],
+        out_specs=vmem,
+        scratch_shapes=[
+            pltpu.VMEM((CORES * blocks + many + 1, rows, kmers), occurrence.dtype),
+            pltpu.SemaphoreType.DMA((3,)),
+        ],
+        compiler_params=pltpu.CompilerParams(vmem_limit_bytes=60 << 20),
+        name="tiles",
+    )(pick, read_block, occurrence, sibling, incoming)
+
+
+def shards(occurrence, block_owner, read_block, slot_order):
+    devices = lax.axis_size("dev")
+    blocks = occurrence.shape[0]
+    lane = 2 * (2 * blocks // devices) + 2
+    swap = [(d, d ^ 1) for d in range(devices)]
+    sibling = lax.ppermute(occurrence, "dev", swap)
+    table = group_table(block_owner, slot_order)
+    fits = fullest_lane(table, blocks) <= CORES * lane
+    return lax.cond(
+        fits,
+        lambda: direct(occurrence, sibling, read_block, table, lane),
+        lambda: exchange_by_owner(occurrence, block_owner, read_block, slot_order),
+    )
+
+
 def solution(mesh):
     placed = (P("dev", None, None), P("dev", None), P("dev"), P("dev", None))
     return jax.shard_map(

time: 500 us -> 312 us (0.62)
  waiting for transfers between devices: 370 us -> 230 us
  local copies, waits for them, and re-layouts: 66.3 us -> 2.12 us
  blocking collectives: 0 us -> 41.6 us
  matrix products: 36.9 us -> 1.09 us
  Pallas kernels: 0 us -> 22.2 us
  starting transfers between devices: 17.7 us -> 5.04 us
    all_to_all x3 -> x1, waiting for transfers between devices: 370 us -> 230 us  [direct(): lax.all_to_all(outgoing, 'dev', split_axis=0, concat_axis=0, tiled=True)]
    unnamed x0 -> x1, blocking collectives: none -> 41.6 us
    gather x4 -> x0, local copies, waits for them, and re-layouts: 38.3 us -> none  [the longest x2 20 us: shards(): groups[:, others_table].reshape(slot_total, CAP - 1, rows, kmers)]
    dot_general x5 -> x3, matrix products: 36.9 us -> 1.09 us  [the longest x1 0.74 us: fullest_lane(): jnp.einsum('gc,gd->cd', held_chip.astype(jnp.bfloat16), (held > 0).astype...]
    pallas_call x0 -> x2, Pallas kernels: none -> 22.2 us  [the longest x1 15 us: direct(): pl.pallas_call(tile_kernel, out_shape=jax.ShapeDtypeStruct((RB_DEV * rows...]
    reshape x3, local copies, waits for them, and re-layouts: 17.2 us -> 0.85 us  [the longest x1 0.69 us: routes(): return (send.reshape(-1), pick)]
    all_to_all x3 -> x1, starting transfers between devices: 17.7 us -> 4.55 us  [direct(): lax.all_to_all(outgoing, 'dev', split_axis=0, concat_axis=0, tiled=True)]
    another operation x2 -> x0, other arithmetic: 6.06 us -> none  [shards(): partner_full = jnp.stack(stacked, axis=1)]
  transfers between devices with their start and end apart: 3 -> 2, of which waited for: 2 -> 1; matrix products, arithmetic and copies ran while one was open for 9% -> 3% of each run, Pallas kernels for 0% -> 0%
where the time goes in v1:
time: 312 us
  waiting for transfers between devices  230 us (74%)
  blocking collectives  41.6 us (13%)
  Pallas kernels  22.2 us (7%)
  other arithmetic  7.9 us (3%)
  starting transfers between devices  5.04 us (2%)
    all_to_all x1, waiting for transfers between devices, direct(): lax.all_to_all(outgoing, 'dev', split_axis=0, concat_axis=0, tiled=True)  230 us
    unnamed x1, blocking collectives  41.6 us
    pallas_call x1, Pallas kernels, direct(): pl.pallas_call(tile_kernel, out_shape=jax.ShapeDtypeStruct((RB_DEV * rows...  15 us
    pallas_call x1, Pallas kernels, direct(): pl.pallas_call(pack_kernel, out_shape=jax.ShapeDtypeStruct((many, rows, k...  7.22 us
  transfers between devices with their start and end apart: 2, of which 1 were waited for; matrix products, arithmetic and copies ran while one was open for 3% of the time, Pallas kernels for 0%

profile of v1, /device:TPU:0, one launch (start us, length us, event | category | flops | bytes accessed | tf_op | source)
XLA Modules:
  0.0 311.7 jit_solution(16983550857775869083)
XLA Ops:
  0.0 0.5 collective-permute-start
  0.5 0.9 add_dynamic-update-slice_fusion
  1.4 41.6 %all-reduce = s32[6144]{0:T(1024)S(1)} all-reduce(s32[6144]{0:T(1024)S(1)} %add_dynamic-update-slice_fusion), channel_id=2, replica_groups=mesh['dev'=32] {'dev'}, use_global_device_ids=true, to_apply=%add | all-reduce | flops 6144 | bytes 49152
  43.0 0.1 reshape.377
  43.2 0.9 convert_reduce_fusion.1
  44.2 0.7 select_reduce_fusion.6
  44.9 0.1 copy.70
  45.0 0.1 copy.71
  45.1 0.1 copy.68
  45.3 0.1 copy.69
  45.3 2.9 select_reduce_fusion.5
  48.3 0.1 sub.52
  48.4 0.1 gt.45
  48.6 0.1 reshape.344
  48.7 0.2 reduce_sum.114
  48.9 0.7 fusion.52
  50.3 261.2 %conditional.1 = (f32[2048,512]{1,0:T(8,128)}) conditional(s32[]{:T(128)} %convert_element_type.56, (s32[64]{0:T(128)}, s32[64,1]{0,1:T(1,128)}, s32[1,128]{1,0:T(1,128)}, bf16[64,128,128]{2,1,0:T(8,128)(2,1)}, (), /*index=5*/()) %tuple.11, (s32[4,32,32]{2,1,0:T(8,128)S(1)}, bf16[64,128,128]{2,1,0:T(8,128)(2,1)}, ...), branch_computations={%region_6.9_spmd, %region_9.18_spmd} | conditional | flops 2310081280 | bytes 274786048 | solution.py:251
  50.9 0.4 select_reduce_fusion.3
  51.4 0.2 fusion.1
  51.6 0.3 select_reduce_fusion.4
  51.9 0.1 copy.58
  52.0 0.7 reshape.338.send_ref
  52.7 7.2 %pack.1 = bf16[320,128,128]{2,1,0:T(8,128)(2,1)} custom-call(s32[320]{0:T(512)} %reshape.338.send_ref, bf16[64,128,128]{2,1,0:T(8,128)(2,1)} %get-tuple-element.37.own_ref, bf16[64,128,128]{2,1,0:T(8,128)(2,1)S(1)} %get-tuple-element.38.sib_ref), custom_call_target="tpu_custom_call" | custom-call | tf_op jit(solution)/shard_map/cond/branch_1_fun/pack/pallas_call | solution.py:216
  59.9 4.5 %all-to-all-start = ((bf16[320,128,128]{2,1,0:T(8,128)(2,1)}), bf16[320,128,128]{2,1,0:T(8,128)(2,1)}, u32[]{:S(2)}, u32[]{:S(2)}) async-start(bf16[320,128,128]{2,1,0:T(8,128)(2,1)} %pack.1), calls=%async_computation | async-start | bytes 20971520 | tf_op jit(solution)/shard_map/cond/branch_1_fun/all_to_all | solution.py:228
  64.5 0.1 constant_dynamic-slice_fusion
  64.6 0.1 reshape.336
  64.7 0.4 compare_reduce_fusion
  65.0 0.2 fusion.9
  65.2 0.4 fusion
  65.6 0.6 compare_select_fusion.2.pick_ref
  66.1 230.3 %all-to-all-done.got_ref = bf16[320,128,128]{2,1,0:T(8,128)(2,1)} async-done(((bf16[320,128,128]{2,1,0:T(8,128)(2,1)}), bf16[320,128,128]{2,1,0:T(8,128)(2,1)}, u32[]{:S(2)}, u32[]{:S(2)}) %all-to-all-start) | async-done | bytes 10485792 | tf_op jit(solution)/shard_map/cond/branch_1_fun/all_to_all | solution.py:228
  296.5 15.0 %tiles.1 = f32[2048,512]{1,0:T(8,128)} custom-call(s32[256]{0:T(256)} %compare_select_fusion.2.pick_ref, s32[64]{0:T(128)S(1)} %copy-done.4, bf16[64,128,128]{2,1,0:T(8,128)(2,1)S(1)} %copy-done.1, bf16[64,128,128]{2,1,0:T(8,128)(2,1)} %copy-done.2, bf16[320,128,128]{2,1,0:T(8,128)(2,1)} %all-to-all-done.got_ref), custom_call_target="tpu_custom_call" | custom-call | tf_op jit(solution)/shard_map/cond/branch_1_fun/tiles/pallas_call | solution.py:229
  (35 shorter events, 0.7 us)
Async XLA Ops:
  0.0 50.3 %collective-permute-start = (bf16[64,128,128]{2,1,0:T(8,128)(2,1)}, bf16[64,128,128]{2,1,0:T(8,128)(2,1)S(1)}, u32[]{:S(2)}, u32[]{:S(2)}) collective-permute-start(bf16[64,128,128]{2,1,0:T(8,128)(2,1)} %param.8), channel_id=1, source_target_pairs={{0,1},{1,0},{2,3},{3,2},{4,5},{5,4},{6,7},{7,6},{8,9},{9,8},{10,11... | collective-permute-start | bytes 6291464 | tf_op jit(solution)/shard_map/ppermute | solution.py:248
  50.5 2.2 copy-start.2
  59.9 236.6 %copy-start.1 = (bf16[64,128,128]{2,1,0:T(8,128)(2,1)S(1)}, bf16[64,128,128]{2,1,0:T(8,128)(2,1)}, u32[]{:S(2)}) copy-start(bf16[64,128,128]{2,1,0:T(8,128)(2,1)} %get-tuple-element.37.own_ref) | copy-start | bytes 6291460 | tf_op jit(solution)/shard_map/cond
  59.9 236.6 %copy-start.4 = (s32[64]{0:T(128)S(1)}, s32[64]{0:T(128)}, u32[]{:S(2)}) copy-start(s32[64]{0:T(128)} %get-tuple-element.36.read_ref) | copy-start | bytes 772 | tf_op jit(solution)/shard_map/cond
  59.9 236.5 %all-to-all-start = ((bf16[320,128,128]{2,1,0:T(8,128)(2,1)}), bf16[320,128,128]{2,1,0:T(8,128)(2,1)}, u32[]{:S(2)}, u32[]{:S(2)}) async-start(bf16[320,128,128]{2,1,0:T(8,128)(2,1)} %pack.1), calls=%async_computation | async-start | bytes 20971520 | tf_op jit(solution)/shard_map/cond/branch_1_fun/all_to_all | solution.py:228

commit v2 on v1

v2 whole, which is shorter than its diff:
```python
import functools
import jax
import jax.numpy as jnp
import numpy as np
from jax import lax
from jax.experimental import pallas as pl
from jax.experimental.pallas import tpu as pltpu
from jax.sharding import PartitionSpec as P

CAP = 4
RB_DEV = 16
CORES = 2
HALVES = 2
FAMILY = CORES * HALVES


def i32(x):
    return x.astype(jnp.int32)


def iota(*shape, axis):
    return lax.broadcasted_iota(jnp.int32, shape, axis)


def group_table(block_owner, slot_order):
    devices = lax.axis_size("dev")
    blocks = block_owner.shape[0]
    slots = slot_order.shape[1]
    per_pair = slots // devices
    mine = jnp.concatenate([block_owner[:, 0], slot_order[0]])
    everyone = lax.all_gather(mine, "dev", axis=0)
    owners, order = everyone[:, :blocks], everyone[:, blocks:]
    earlier = iota(blocks, blocks, axis=1) < iota(blocks, blocks, axis=0)
    same = owners[:, :, None] == owners[:, None, :]
    rank = jnp.sum(i32(same & earlier[None]), axis=2)
    key = owners * per_pair + rank
    number = iota(devices, blocks, axis=0) * blocks + iota(devices, blocks, axis=1) + 1
    hit = key[:, :, None] == iota(1, 1, slots, axis=2)
    holder = jnp.sum(jnp.where(hit, number[:, :, None], 0), axis=1)
    holder = holder.reshape(devices, devices, per_pair).transpose(1, 0, 2).reshape(devices, slots)
    turned = order.reshape(devices, slots // CAP, CAP).transpose(2, 0, 1)
    hit = turned[:, :, :, None] == iota(1, 1, 1, slots, axis=3)
    table = jnp.sum(jnp.where(hit, holder[None, :, None, :], 0), axis=3)
    return table.reshape(CAP, devices * slots // CAP)


def fullest_lane(table, blocks):
    devices = lax.axis_size("dev")
    families = devices // FAMILY
    source = jnp.where(table > 0, (table - 1) // blocks, -1)
    named = source[:, :, None] == iota(1, 1, devices, axis=2)
    held = jnp.sum(i32(named), axis=0)
    held_family = jnp.sum(held.reshape(-1, HALVES, families, CORES), axis=(1, 3))
    demand = jnp.einsum(
        "gf,gd->fd",
        held_family.astype(jnp.bfloat16),
        (held > 0).astype(jnp.bfloat16),
        preferred_element_type=jnp.float32,
    )
    f, d = iota(families, devices, axis=0), iota(families, devices, axis=1)
    return jnp.max(jnp.where(f != d // CORES % families, demand, 0.0))


def routes(table, blocks, lane):
    devices = lax.axis_size("dev")
    families = devices // FAMILY
    half_devices = devices // HALVES
    many = FAMILY * blocks
    me = lax.axis_index("dev")
    half, family, core = me // half_devices, me // CORES % families, me % CORES
    x = jnp.arange(many, dtype=jnp.int32)
    x_half, x_core, x_block = x // (CORES * blocks), x // blocks % CORES, x % blocks
    ids = (((x_half * families + family) * CORES + x_core) * blocks + x_block + 1)[:, None]
    inside = (table[0][None] == ids) | (table[1][None] == ids)
    for j in range(2, CAP):
        inside = inside | (table[j][None] == ids)
    partners = jnp.stack(
        [jnp.sum(jnp.where(inside, table[j][None], 0), axis=1) for j in range(CAP)]
    )
    source = jnp.where(partners > 0, (partners - 1) // blocks, -1)
    target = iota(1, half_devices, axis=1) + half * half_devices
    named = source[:, :, None] == target[None]
    need = jnp.any(named, axis=0) & (target // CORES % families != family)
    before = (iota(many, many, axis=1) < iota(many, many, axis=0)).astype(jnp.bfloat16)
    rank = i32(jnp.dot(before, need.astype(jnp.bfloat16), preferred_element_type=jnp.float32))
    rank = jnp.where(need, rank, -1).T
    local = (i32(x_half != half) * CORES + i32(x_core != core)) * blocks + x_block

    begin = half * CORES * blocks + core * blocks
    own = lax.dynamic_slice(partners, (0, begin), (CAP, blocks)).reshape(-1)
    total = devices * blocks
    match = own[:, None] == iota(1, total, axis=1) + 1
    wanted = jnp.any(match, axis=0).reshape(HALVES, families, CORES * blocks)
    wanted = wanted.transpose(1, 0, 2).reshape(families, many)
    arrived = i32(
        jnp.dot(wanted.astype(jnp.bfloat16), before.T, preferred_element_type=jnp.float32)
    )
    f = iota(families, many, axis=0)
    empty = many + half_devices * lane

    def send(turn):
        spot = (turn * lane + iota(1, lane, 1, axis=1)) * CORES + core
        return jnp.sum(jnp.where(rank[:, None, :] == spot, local[None, None, :], 0), axis=2).reshape(-1)

    def pick(turn):
        now = arrived - turn * lane * CORES
        there = many + (f * CORES + now % CORES) * lane + now // CORES
        there = jnp.where((now >= 0) & (now < lane * CORES), there, empty)
        place = jnp.where(f == family, jnp.where(turn == 0, local, empty)[None, :], there)
        place = place.reshape(families, HALVES, CORES * blocks).transpose(1, 0, 2).reshape(1, total)
        found = jnp.sum(jnp.where(match, place, 0), axis=1)
        return jnp.where(own > 0, found, empty)

    return send, pick


def fill(near, held, sems):
    blocks = near[0].shape[0]
    copies = [
        pltpu.make_async_copy(ref, held.at[pl.ds(i * blocks, blocks)], sems.at[i])
        for i, ref in enumerate(near)
    ]
    for copy in copies:
        copy.start()
    return copies


def pack_kernel(send_ref, a_ref, b_ref, c_ref, d_ref, out_ref, held, sems):
    for copy in fill((a_ref, b_ref, c_ref, d_ref), held, sems):
        copy.wait()

    def step(i, _):
        out_ref[i] = held[send_ref[i]]
        return 0

    lax.fori_loop(0, out_ref.shape[0], step, 0, unroll=4)


def tile_kernel(pick_ref, read_ref, a_ref, b_ref, c_ref, d_ref, got_ref, out_ref, held, sems):
    blocks, rows = a_ref.shape[:2]
    near, many = FAMILY * blocks, got_ref.shape[0]
    copies = fill((a_ref, b_ref, c_ref, d_ref), held, sems)
    last = pltpu.make_async_copy(got_ref, held.at[pl.ds(near, many)], sems.at[FAMILY])
    last.start()
    held[near + many] = jnp.zeros(held.shape[1:], held.dtype)
    out_ref[...] = jnp.zeros_like(out_ref)
    for copy in copies:
        copy.wait()
    last.wait()

    def step(b, _):
        others = jnp.concatenate([held[pick_ref[j * blocks + b]] for j in range(CAP)], axis=0)
        tile = lax.dot_general(
            held[b], others, (((1,), (1,)), ((), ())), preferred_element_type=jnp.float32
        )
        where = pl.ds(pl.multiple_of(read_ref[b] * rows, rows), rows)
        out_ref[where, :] += tile.astype(jnp.bfloat16).astype(jnp.float32)
        return 0

    lax.fori_loop(0, blocks, step, 0, unroll=2)


SMEM = pl.BlockSpec(memory_space=pltpu.SMEM)
HBM = pl.BlockSpec(memory_space=pl.ANY)
VMEM = pl.BlockSpec(memory_space=pltpu.VMEM)


def pack(send, near):
    blocks, rows, kmers = near[0].shape
    return pl.pallas_call(
        pack_kernel,
        out_shape=jax.ShapeDtypeStruct((send.shape[0], rows, kmers), near[0].dtype),
        in_specs=[SMEM] + [HBM] * FAMILY,
        out_specs=VMEM,
        scratch_shapes=[
            pltpu.VMEM((FAMILY * blocks, rows, kmers), near[0].dtype),
            pltpu.SemaphoreType.DMA((FAMILY,)),
        ],
        compiler_params=pltpu.CompilerParams(vmem_limit_bytes=60 << 20),
        name="pack",
    )(send, *near)


def tiles(pick, read_block, near, got):
    blocks, rows, kmers = near[0].shape
    return pl.pallas_call(
        tile_kernel,
        out_shape=jax.ShapeDtypeStruct((RB_DEV * rows, CAP * rows), jnp.float32),
        in_specs=[SMEM, SMEM] + [HBM] * (FAMILY + 1),
        out_specs=VMEM,
        scratch_shapes=[
            pltpu.VMEM((FAMILY * blocks + got.shape[0] + 1, rows, kmers), got.dtype),
            pltpu.SemaphoreType.DMA((FAMILY + 1,)),
        ],
        compiler_params=pltpu.CompilerParams(vmem_limit_bytes=60 << 20),
        name="tiles",
    )(pick, read_block, *near, got)


def shards(occurrence, block_owner, read_block, slot_order):
    devices = lax.axis_size("dev")
    blocks = occurrence.shape[0]
    half_devices = devices // HALVES
    lane = 2 * (2 * blocks // devices) + 7
    swap = [(d, d ^ 1) for d in range(devices)]
    across = [(d, (d + half_devices) % devices) for d in range(devices)]
    groups = np.arange(devices).reshape(HALVES, half_devices).tolist()
    far = lax.ppermute(occurrence, "dev", across)
    sibling = lax.ppermute(occurrence, "dev", swap)
    near = (occurrence, sibling, far, lax.ppermute(far, "dev", swap))
    table = group_table(block_owner, slot_order)
    most = i32(fullest_lane(table, blocks))
    turns = (most + CORES * lane - 1) // (CORES * lane)
    send, pick = routes(table, blocks, lane)

    def one(turn):
        out = pack(send(turn), near)
        got = lax.all_to_all(
            out, "dev", split_axis=0, concat_axis=0, axis_index_groups=groups, tiled=True
        )
        return tiles(pick(turn), read_block, near, got)

    def more(carry):
        turn, margin = carry
        return turn + 1, margin + one(turn)

    first = one(jnp.int32(0))
    return lax.while_loop(lambda carry: carry[0] < turns, more, (jnp.int32(1), first))[1]


def solution(mesh):
    placed = (P("dev", None, None), P("dev", None), P("dev"), P("dev", None))
    return jax.shard_map(
        shards, mesh=mesh, in_specs=placed, out_specs=P("dev", None), check_vma=False
    )
```

time: 312 us -> 276 us (0.88)
  waiting for transfers between devices: 230 us -> 118 us
  blocking collectives: 41.6 us -> 112 us
  starting transfers between devices: 5.04 us -> 8.98 us
    all_to_all x1, waiting for transfers between devices: 230 us -> 118 us  [one(): lax.all_to_all(out, 'dev', split_axis=0, concat_axis=0, axis_index_groups...]
    unnamed x1, blocking collectives: 41.6 us -> 112 us
    ppermute x0 -> x2, starting transfers between devices: none -> 4.14 us  [the longest x1 4.06 us: shards(): far = lax.ppermute(occurrence, 'dev', across)]
  transfers between devices with their start and end apart: 2 -> 4, of which waited for: 1 -> 1; matrix products, arithmetic and copies ran while one was open for 3% -> 4% of each run, Pallas kernels for 0% -> 0%
where the time goes in v2:
time: 276 us; the launch traced here: 275 us
  waiting for transfers between devices  118 us (43%)
  blocking collectives  112 us (41%)
  Pallas kernels  23.1 us (8%)
  starting transfers between devices  8.98 us (3%)
  other arithmetic  8.61 us (3%)
    all_to_all x1, waiting for transfers between devices, one(): lax.all_to_all(out, 'dev', split_axis=0, concat_axis=0, axis_index_groups...  118 us
    unnamed x1, blocking collectives  112 us
    pallas_call x1, Pallas kernels, tiles(): pl.pallas_call(tile_kernel, out_shape=jax.ShapeDtypeStruct((RB_DEV * rows...  15.5 us
    pallas_call x1, Pallas kernels, pack(): pl.pallas_call(pack_kernel, out_shape=jax.ShapeDtypeStruct((send.shape[0]...  7.58 us
  transfers between devices with their start and end apart: 4, of which 1 were waited for; matrix products, arithmetic and copies ran while one was open for 4% of the time, Pallas kernels for 0%

profile of v2, /device:TPU:0, one launch (start us, length us, event | category | flops | bytes accessed | tf_op | source)
XLA Modules:
  0.0 274.7 jit_solution(11400476928639038514)
XLA Ops:
  0.0 4.1 %collective-permute-start.1 = (bf16[64,128,128]{2,1,0:T(8,128)(2,1)}, bf16[64,128,128]{2,1,0:T(8,128)(2,1)S(1)}, u32[]{:S(2)}, u32[]{:S(2)}) collective-permute-start(bf16[64,128,128]{2,1,0:T(8,128)(2,1)} %a_ref.3), channel_id=1, source_target_pairs={{0,16},{1,17},{2,18},{3,19},{4,20},{5,21},{6,22},{7,23},{8,24},{9,... | collective-permute-start | bytes 6291464 | tf_op jit(solution)/shard_map/ppermute | solution.py:208
  4.1 0.8 add_dynamic-update-slice_fusion
  4.9 112.3 %all-reduce = s32[6144]{0:T(1024)S(1)} all-reduce(s32[6144]{0:T(1024)S(1)} %add_dynamic-update-slice_fusion), channel_id=2, replica_groups=mesh['dev'=32] {'dev'}, use_global_device_ids=true, to_apply=%add | all-reduce | flops 6144 | bytes 49152
  117.3 0.1 reshape.437
  117.4 0.9 convert_reduce_fusion
  118.5 0.7 select_reduce_fusion.7
  119.3 0.1 copy.28
  119.3 0.1 copy.29
  119.5 0.1 copy.26
  119.6 0.1 copy.27
  119.7 2.9 %select_reduce_fusion.2 = s32[4,32,32]{2,1,0:T(8,128)S(1)} fusion(s32[32,128]{1,0:T(8,128)S(1)} %copy.30, s32[4,32,32]{2,1,0:T(8,128)S(1)} %copy.27), kind=kLoop, calls=%fused_computation.56 | loop fusion | flops 1568768 | bytes 49152 | tf_op jit(solution)/shard_map/reduce_sum | solution.py:43
  123.0 0.9 select_reduce_fusion.6
  124.0 0.1 compare_reduce_fusion.1
  124.0 0.2 fusion.28
  124.2 0.4 select_reduce_fusion.8
  124.6 0.1 copy.31
  124.7 0.7 reshape.434.send_ref
  125.4 7.6 %pack.5 = bf16[240,128,128]{2,1,0:T(8,128)(2,1)} custom-call(s32[240]{0:T(256)} %reshape.434.send_ref, bf16[64,128,128]{2,1,0:T(8,128)(2,1)} %a_ref.3, bf16[64,128,128]{2,1,0:T(8,128)(2,1)} %collective-permute-done.b_ref, bf16[64,128,128]{2,1,0:T(8,128)(2,1)S(1)} %collective-permute-done.1.c_ref, bf16[64,128,128]{2,1,0:T(8,128)(2,1)} %collective-permute-done.2.d_ref), custom_call_target="tpu_custom_call" | custom-call | tf_op jit(solution)/shard_map/pack/pallas_call | solution.py:170
  133.0 4.8 %all-to-all-start.1 = ((bf16[240,128,128]{2,1,0:T(8,128)(2,1)}), bf16[240,128,128]{2,1,0:T(8,128)(2,1)}, u32[]{:S(2)}, u32[]{:S(2)}) async-start(bf16[240,128,128]{2,1,0:T(8,128)(2,1)} %pack.5), calls=%async_computation.1 | async-start | bytes 15728640 | tf_op jit(solution)/shard_map/all_to_all | solution.py:218
  137.9 0.1 sub.95
  138.0 0.1 gt.45
  138.3 0.1 reduce_sum.133
  138.4 0.7 fusion.29
  139.8 0.1 constant_dynamic-slice_fusion
  139.9 0.1 reshape.430
  140.0 0.4 compare_reduce_fusion
  140.4 0.2 convolution_convert_fusion.1
  140.5 0.1 fusion.43
  140.6 0.4 fusion.27
  141.0 0.6 compare_select_fusion.10.pick_ref
  141.6 117.6 %all-to-all-done.1.got_ref = bf16[240,128,128]{2,1,0:T(8,128)(2,1)} async-done(((bf16[240,128,128]{2,1,0:T(8,128)(2,1)}), bf16[240,128,128]{2,1,0:T(8,128)(2,1)}, u32[]{:S(2)}, u32[]{:S(2)}) %all-to-all-start.1) | async-done | bytes 7864352 | tf_op jit(solution)/shard_map/all_to_all | solution.py:218
  259.2 15.5 %tiles.5 = f32[2048,512]{1,0:T(8,128)} custom-call(s32[256]{0:T(256)} %compare_select_fusion.10.pick_ref, s32[64]{0:T(128)S(1)} %copy-done.2, bf16[64,128,128]{2,1,0:T(8,128)(2,1)S(1)} %copy-done, bf16[64,128,128]{2,1,0:T(8,128)(2,1)} %collective-permute-done.b_ref, bf16[64,128,128]{2,1,0:T(8,128)(2,1)} %copy-done.1, ...), custom_call_target="tpu_custom_call" | custom-call | tf_op jit(solution)/shard_map/tiles/pallas_call | solution.py:186
  (41 shorter events, 0.9 us)
Async XLA Ops:
  0.0 118.4 %collective-permute-start.1 = (bf16[64,128,128]{2,1,0:T(8,128)(2,1)}, bf16[64,128,128]{2,1,0:T(8,128)(2,1)S(1)}, u32[]{:S(2)}, u32[]{:S(2)}) collective-permute-start(bf16[64,128,128]{2,1,0:T(8,128)(2,1)} %a_ref.3), channel_id=1, source_target_pairs={{0,16},{1,17},{2,18},{3,19},{4,20},{5,21},{6,22},{7,23},{8,24},{9,... | collective-permute-start | bytes 6291464 | tf_op jit(solution)/shard_map/ppermute | solution.py:208
  4.1 121.3 %collective-permute-start = (bf16[64,128,128]{2,1,0:T(8,128)(2,1)}, bf16[64,128,128]{2,1,0:T(8,128)(2,1)}, u32[]{:S(2)}, u32[]{:S(2)}) collective-permute-start(bf16[64,128,128]{2,1,0:T(8,128)(2,1)} %a_ref.3), channel_id=1, source_target_pairs={{0,1},{1,0},{2,3},{3,2},{4,5},{5,4},{6,7},{7,6},{8,9},{9,8},{10,11... | collective-permute-start | bytes 6291464 | tf_op jit(solution)/shard_map/ppermute | solution.py:209
  118.4 7.0 %copy-start.1 = (bf16[64,128,128]{2,1,0:T(8,128)(2,1)}, bf16[64,128,128]{2,1,0:T(8,128)(2,1)S(1)}, u32[]{:S(2)}) copy-start(bf16[64,128,128]{2,1,0:T(8,128)(2,1)S(1)} %collective-permute-done.1.c_ref) | copy-start | bytes 6291460
  118.4 7.0 %collective-permute-start.2 = (bf16[64,128,128]{2,1,0:T(8,128)(2,1)S(1)}, bf16[64,128,128]{2,1,0:T(8,128)(2,1)}, u32[]{:S(2)}, u32[]{:S(2)}) collective-permute-start(bf16[64,128,128]{2,1,0:T(8,128)(2,1)S(1)} %collective-permute-done.1.c_ref), channel_id=1, source_target_pairs={{0,1},{1,0},{2,3},{3,2},{4,5},{5,4},{6,7},{7,6},{8,9},{9,8},{10,11... | collective-permute-start | bytes 6291464 | tf_op jit(solution)/shard_map/ppermute | solution.py:210
  133.0 126.2 %copy-start = (bf16[64,128,128]{2,1,0:T(8,128)(2,1)S(1)}, bf16[64,128,128]{2,1,0:T(8,128)(2,1)}, u32[]{:S(2)}) copy-start(bf16[64,128,128]{2,1,0:T(8,128)(2,1)} %a_ref.3) | copy-start | bytes 6291460
  133.0 126.2 %copy-start.2 = (s32[64]{0:T(128)S(1)}, s32[64]{0:T(128)}, u32[]{:S(2)}) copy-start(s32[64]{0:T(128)} %read_ref.1) | copy-start | bytes 772
  133.0 126.2 %all-to-all-start.1 = ((bf16[240,128,128]{2,1,0:T(8,128)(2,1)}), bf16[240,128,128]{2,1,0:T(8,128)(2,1)}, u32[]{:S(2)}, u32[]{:S(2)}) async-start(bf16[240,128,128]{2,1,0:T(8,128)(2,1)} %pack.5), calls=%async_computation.1 | async-start | bytes 15728640 | tf_op jit(solution)/shard_map/all_to_all | solution.py:218

commit v3 on v2

--- a/solution.py
+++ b/solution.py
@@ -22,14 +22,10 @@
     return lax.broadcasted_iota(jnp.int32, shape, axis)
 
 
-def group_table(block_owner, slot_order):
-    devices = lax.axis_size("dev")
-    blocks = block_owner.shape[0]
-    slots = slot_order.shape[1]
+def group_table(owners, order):
+    devices, blocks = owners.shape
+    slots = order.shape[1]
     per_pair = slots // devices
-    mine = jnp.concatenate([block_owner[:, 0], slot_order[0]])
-    everyone = lax.all_gather(mine, "dev", axis=0)
-    owners, order = everyone[:, :blocks], everyone[:, blocks:]
     earlier = iota(blocks, blocks, axis=1) < iota(blocks, blocks, axis=0)
     same = owners[:, :, None] == owners[:, None, :]
     rank = jnp.sum(i32(same & earlier[None]), axis=2)
@@ -47,18 +43,19 @@
 def fullest_lane(table, blocks):
     devices = lax.axis_size("dev")
     families = devices // FAMILY
+    chips = devices // CORES
     source = jnp.where(table > 0, (table - 1) // blocks, -1)
     named = source[:, :, None] == iota(1, 1, devices, axis=2)
     held = jnp.sum(i32(named), axis=0)
-    held_family = jnp.sum(held.reshape(-1, HALVES, families, CORES), axis=(1, 3))
+    held_chip = jnp.sum(held.reshape(-1, chips, CORES), axis=2)
     demand = jnp.einsum(
-        "gf,gd->fd",
-        held_family.astype(jnp.bfloat16),
+        "gc,gd->cd",
+        held_chip.astype(jnp.bfloat16),
         (held > 0).astype(jnp.bfloat16),
         preferred_element_type=jnp.float32,
     )
-    f, d = iota(families, devices, axis=0), iota(families, devices, axis=1)
-    return jnp.max(jnp.where(f != d // CORES % families, demand, 0.0))
+    c, d = iota(chips, devices, axis=0), iota(chips, devices, axis=1)
+    return jnp.max(jnp.where(c % families != d // CORES % families, demand, 0.0))
 
 
 def routes(table, blocks, lane):
@@ -81,7 +78,9 @@
     target = iota(1, half_devices, axis=1) + half * half_devices
     named = source[:, :, None] == target[None]
     need = jnp.any(named, axis=0) & (target // CORES % families != family)
-    before = (iota(many, many, axis=1) < iota(many, many, axis=0)).astype(jnp.bfloat16)
+    row, column = iota(many, many, axis=0), iota(many, many, axis=1)
+    same_chip = row // (CORES * blocks) == column // (CORES * blocks)
+    before = ((column < row) & same_chip).astype(jnp.bfloat16)
     rank = i32(jnp.dot(before, need.astype(jnp.bfloat16), preferred_element_type=jnp.float32))
     rank = jnp.where(need, rank, -1).T
     local = (i32(x_half != half) * CORES + i32(x_core != core)) * blocks + x_block
@@ -96,15 +95,18 @@
         jnp.dot(wanted.astype(jnp.bfloat16), before.T, preferred_element_type=jnp.float32)
     )
     f = iota(families, many, axis=0)
-    empty = many + half_devices * lane
-
-    def send(turn):
+    part = i32(iota(families, many, axis=1) // (CORES * blocks) != half)
+    empty = many + HALVES * half_devices * lane
+
+    def send(turn, far):
         spot = (turn * lane + iota(1, lane, 1, axis=1)) * CORES + core
-        return jnp.sum(jnp.where(rank[:, None, :] == spot, local[None, None, :], 0), axis=2).reshape(-1)
+        chosen = jnp.where((x_half != half) == far, local % (CORES * blocks), 0)
+        hit = (rank[:, None, :] == spot) & ((x_half != half) == far)
+        return jnp.sum(jnp.where(hit, chosen[None, None, :], 0), axis=2).reshape(-1)
 
     def pick(turn):
         now = arrived - turn * lane * CORES
-        there = many + (f * CORES + now % CORES) * lane + now // CORES
+        there = (part * half_devices + f * CORES + now % CORES) * lane + now // CORES + many
         there = jnp.where((now >= 0) & (now < lane * CORES), there, empty)
         place = jnp.where(f == family, jnp.where(turn == 0, local, empty)[None, :], there)
         place = place.reshape(families, HALVES, CORES * blocks).transpose(1, 0, 2).reshape(1, total)
@@ -125,8 +127,8 @@
     return copies
 
 
-def pack_kernel(send_ref, a_ref, b_ref, c_ref, d_ref, out_ref, held, sems):
-    for copy in fill((a_ref, b_ref, c_ref, d_ref), held, sems):
+def pack_kernel(send_ref, a_ref, b_ref, out_ref, held, sems):
+    for copy in fill((a_ref, b_ref), held, sems):
         copy.wait()
 
     def step(i, _):
@@ -136,17 +138,19 @@
     lax.fori_loop(0, out_ref.shape[0], step, 0, unroll=4)
 
 
-def tile_kernel(pick_ref, read_ref, a_ref, b_ref, c_ref, d_ref, got_ref, out_ref, held, sems):
-    blocks, rows = a_ref.shape[:2]
-    near, many = FAMILY * blocks, got_ref.shape[0]
-    copies = fill((a_ref, b_ref, c_ref, d_ref), held, sems)
-    last = pltpu.make_async_copy(got_ref, held.at[pl.ds(near, many)], sems.at[FAMILY])
-    last.start()
-    held[near + many] = jnp.zeros(held.shape[1:], held.dtype)
+def tile_kernel(pick_ref, read_ref, *refs):
+    near, got, (out_ref, held, sems) = refs[:FAMILY], refs[FAMILY:-3], refs[-3:]
+    blocks, rows = near[0].shape[:2]
+    base, many = FAMILY * blocks, got[0].shape[0]
+    copies = fill(near, held, sems)
+    for i, ref in enumerate(got):
+        into = held.at[pl.ds(base + i * many, many)]
+        copies.append(pltpu.make_async_copy(ref, into, sems.at[FAMILY + i]))
+        copies[-1].start()
+    held[base + HALVES * many] = jnp.zeros(held.shape[1:], held.dtype)
     out_ref[...] = jnp.zeros_like(out_ref)
     for copy in copies:
         copy.wait()
-    last.wait()
 
     def step(b, _):
         others = jnp.concatenate([held[pick_ref[j * blocks + b]] for j in range(CAP)], axis=0)
@@ -170,11 +174,11 @@
     return pl.pallas_call(
         pack_kernel,
         out_shape=jax.ShapeDtypeStruct((send.shape[0], rows, kmers), near[0].dtype),
-        in_specs=[SMEM] + [HBM] * FAMILY,
+        in_specs=[SMEM] + [HBM] * CORES,
         out_specs=VMEM,
         scratch_shapes=[
-            pltpu.VMEM((FAMILY * blocks, rows, kmers), near[0].dtype),
-            pltpu.SemaphoreType.DMA((FAMILY,)),
+            pltpu.VMEM((CORES * blocks, rows, kmers), near[0].dtype),
+            pltpu.SemaphoreType.DMA((CORES,)),
         ],
         compiler_params=pltpu.CompilerParams(vmem_limit_bytes=60 << 20),
         name="pack",
@@ -183,48 +187,131 @@
 
 def tiles(pick, read_block, near, got):
     blocks, rows, kmers = near[0].shape
+    total = FAMILY * blocks + HALVES * got[0].shape[0] + 1
     return pl.pallas_call(
         tile_kernel,
         out_shape=jax.ShapeDtypeStruct((RB_DEV * rows, CAP * rows), jnp.float32),
-        in_specs=[SMEM, SMEM] + [HBM] * (FAMILY + 1),
+        in_specs=[SMEM, SMEM] + [HBM] * (FAMILY + HALVES),
         out_specs=VMEM,
         scratch_shapes=[
-            pltpu.VMEM((FAMILY * blocks + got.shape[0] + 1, rows, kmers), got.dtype),
-            pltpu.SemaphoreType.DMA((FAMILY + 1,)),
+            pltpu.VMEM((total, rows, kmers), near[0].dtype),
+            pltpu.SemaphoreType.DMA((FAMILY + HALVES,)),
         ],
         compiler_params=pltpu.CompilerParams(vmem_limit_bytes=60 << 20),
         name="tiles",
-    )(pick, read_block, *near, got)
+    )(pick, read_block, *near, *got)
+
+
+def everyone_kernel(devices, row_ref, out_ref, send_sems, recv_sems):
+    me = lax.axis_index("dev")
+    out_ref[me] = row_ref[...]
+    copies = []
+    for k in range(1, devices):
+        copies.append(
+            pltpu.make_async_remote_copy(
+                src_ref=row_ref,
+                dst_ref=out_ref.at[me],
+                send_sem=send_sems.at[k],
+                recv_sem=recv_sems.at[k],
+                device_id=(lax.rem(me + k, devices),),
+                device_id_type=pl.DeviceIdType.MESH,
+            )
+        )
+        copies[-1].start()
+    for copy in copies:
+        copy.wait()
+
+
+def gather_rows(row):
+    devices = lax.axis_size("dev")
+    return pl.pallas_call(
+        functools.partial(everyone_kernel, devices),
+        out_shape=jax.ShapeDtypeStruct((devices,) + row.shape, row.dtype),
+        in_specs=[VMEM],
+        out_specs=VMEM,
+        scratch_shapes=[pltpu.SemaphoreType.DMA((devices,))] * 2,
+        compiler_params=pltpu.CompilerParams(has_side_effects=True),
+        name="gather_rows",
+    )(row)
+
+
+def flipped(value, mask):
+    bit = 1
+    while bit <= mask:
+        if mask & bit:
+            value = value + bit - 2 * bit * (value // bit % 2)
+        bit *= 2
+    return value
+
+
+def exchange_kernel(devices, lane, out_ref, got_ref, send_sems, recv_sems):
+    me = lax.axis_index("dev")
+    count = devices // HALVES
+    spot = me % count
+    copies = []
+    for k in range(CORES, count):
+        to = flipped(spot, k)
+        copies.append(
+            pltpu.make_async_remote_copy(
+                src_ref=out_ref.at[pl.ds(to * lane, lane)],
+                dst_ref=got_ref.at[pl.ds(spot * lane, lane)],
+                send_sem=send_sems.at[k],
+                recv_sem=recv_sems.at[k],
+                device_id=(me - spot + to,),
+                device_id_type=pl.DeviceIdType.MESH,
+            )
+        )
+        copies[-1].start()
+    for copy in copies:
+        copy.wait()
+
+
+def exchange(out, lane):
+    devices = lax.axis_size("dev")
+    count = devices // HALVES
+    return pl.pallas_call(
+        functools.partial(exchange_kernel, devices, lane),
+        out_shape=jax.ShapeDtypeStruct(out.shape, out.dtype),
+        in_specs=[HBM],
+        out_specs=HBM,
+        scratch_shapes=[pltpu.SemaphoreType.DMA((count,))] * 2,
+        compiler_params=pltpu.CompilerParams(has_side_effects=True),
+        cost_estimate=pl.CostEstimate(
+            flops=0, bytes_accessed=32 * out.size * out.dtype.itemsize, transcendentals=0
+        ),
+        name="exchange",
+    )(out)
 
 
 def shards(occurrence, block_owner, read_block, slot_order):
     devices = lax.axis_size("dev")
     blocks = occurrence.shape[0]
-    half_devices = devices // HALVES
-    lane = 2 * (2 * blocks // devices) + 7
+    slots = slot_order.shape[1]
+    lane = 2 * (2 * blocks // devices) + 1
     swap = [(d, d ^ 1) for d in range(devices)]
-    across = [(d, (d + half_devices) % devices) for d in range(devices)]
-    groups = np.arange(devices).reshape(HALVES, half_devices).tolist()
-    far = lax.ppermute(occurrence, "dev", across)
-    sibling = lax.ppermute(occurrence, "dev", swap)
-    near = (occurrence, sibling, far, lax.ppermute(far, "dev", swap))
-    table = group_table(block_owner, slot_order)
+    across = [(d, (d + devices // HALVES) % devices) for d in range(devices)]
+    row = jnp.stack([jnp.pad(block_owner[:, 0], (0, slots - blocks)), slot_order[0]])
+    everyone = gather_rows(row)
+    everyone, mine = lax.optimization_barrier((everyone, occurrence))
+    far = lax.ppermute(mine, "dev", across)
+    sibling = lax.ppermute(mine, "dev", swap)
+    table = group_table(everyone[:, 0, :blocks], everyone[:, 1])
     most = i32(fullest_lane(table, blocks))
     turns = (most + CORES * lane - 1) // (CORES * lane)
     send, pick = routes(table, blocks, lane)
-
-    def one(turn):
-        out = pack(send(turn), near)
-        got = lax.all_to_all(
-            out, "dev", split_axis=0, concat_axis=0, axis_index_groups=groups, tiled=True
-        )
-        return tiles(pick(turn), read_block, near, got)
+    got = exchange(pack(send(0, False), (occurrence, sibling)), lane)
+    far, got = lax.optimization_barrier((far, got))
+    distant = (far, lax.ppermute(far, "dev", swap))
+    near = (occurrence, sibling) + distant
+    also = exchange(pack(send(0, True), distant), lane)
+    first = tiles(pick(0), read_block, near, (got, also))
 
     def more(carry):
         turn, margin = carry
-        return turn + 1, margin + one(turn)
-
-    first = one(jnp.int32(0))
+        got = exchange(pack(send(turn, False), near[:CORES]), lane)
+        also = exchange(pack(send(turn, True), distant), lane)
+        return turn + 1, margin + tiles(pick(turn), read_block, near, (got, also))
+
     return lax.while_loop(lambda carry: carry[0] < turns, more, (jnp.int32(1), first))[1]
 
 

time: 276 us -> 231 us (0.84)
  Pallas kernels: 23.1 us -> 213 us
  waiting for transfers between devices: 118 us -> 0.01 us
  blocking collectives: 112 us -> 0 us
  starting transfers between devices: 8.98 us -> 1.22 us
  local copies, waits for them, and re-layouts: 2.08 us -> 5.01 us
    pallas_call x0 -> x3, Pallas kernels: none -> 187 us  [the longest x2 170 us: exchange(): pl.pallas_call(functools.partial(exchange_kernel, devices, lane), out_sha...]
    all_to_all x1 -> x0, waiting for transfers between devices: 118 us -> none  [one(): lax.all_to_all(out, 'dev', split_axis=0, concat_axis=0, axis_index_groups...]
    unnamed x1 -> x0, blocking collectives: 112 us -> none
    all_to_all x1 -> x0, starting transfers between devices: 4.84 us -> none  [one(): lax.all_to_all(out, 'dev', split_axis=0, concat_axis=0, axis_index_groups...]
    pallas_call x1 -> x2, Pallas kernels: 7.58 us -> 10.6 us  [pack(): pl.pallas_call(pack_kernel, out_shape=jax.ShapeDtypeStruct((send.shape[0]...]
    ppermute x3, starting transfers between devices: 4.14 us -> 1.22 us  [the longest x1 0.75 us: shards(): far = lax.ppermute(mine, 'dev', across)]
  transfers between devices with their start and end apart: 4 -> 3, of which waited for: 1 -> 0; matrix products, arithmetic and copies ran while one was open for 4% -> 6% of each run, Pallas kernels for 0% -> 47%
where the time goes in v3:
time: 231 us
  Pallas kernels  213 us (92%)
  other arithmetic  9.06 us (4%)
  local copies, waits for them, and re-layouts  5.01 us (2%)
    pallas_call x2, Pallas kernels, exchange(): pl.pallas_call(functools.partial(exchange_kernel, devices, lane), out_sha...  170 us
    pallas_call x1, Pallas kernels, gather_rows(): pl.pallas_call(functools.partial(everyone_kernel, devices), out_shape=jax...  16.2 us
    pallas_call x1, Pallas kernels, tiles(): pl.pallas_call(tile_kernel, out_shape=jax.ShapeDtypeStruct((RB_DEV * rows...  16 us
    pallas_call x2, Pallas kernels, pack(): pl.pallas_call(pack_kernel, out_shape=jax.ShapeDtypeStruct((send.shape[0]...  10.6 us
  transfers between devices with their start and end apart: 3, of which 0 were waited for; matrix products, arithmetic and copies ran while one was open for 6% of the time, Pallas kernels for 47%

profile of v3, /device:TPU:0, one launch (start us, length us, event | category | flops | bytes accessed | tf_op | source)
XLA Modules:
  0.0 230.8 jit_solution(11632410637350816732)
XLA Ops:
  0.0 0.8 pad_bitcast_fusion
  0.8 1.2 pad_add_fusion.1.row_ref
  2.0 16.2 %gather_rows.1 = s32[32,2,128]{2,1,0:T(2,128)} custom-call(s32[2,128]{1,0:T(2,128)} %pad_add_fusion.1.row_ref), custom_call_target="tpu_custom_call" | custom-call | tf_op jit(solution)/shard_map/gather_rows/pallas_call | solution.py:227
  18.2 0.8 collective-permute-start.1
  19.0 0.8 slice.27
  19.8 0.8 slice.26
  20.6 0.9 convert_reduce_fusion
  21.6 0.7 select_reduce_fusion.8
  22.3 0.1 copy.23
  22.4 0.1 copy.24
  22.5 0.1 copy.21
  22.7 2.9 %select_reduce_fusion.3 = s32[4,32,32]{2,1,0:T(8,128)S(1)} fusion(s32[32,128]{1,0:T(8,128)S(1)} %copy.25, s32[4,32,32]{2,1,0:T(8,128)S(1)} %copy.22), kind=kLoop, calls=%fused_computation.71 | loop fusion | flops 1568768 | bytes 49152 | tf_op jit(solution)/shard_map/reduce_sum | solution.py:39
  25.8 0.1 gt.47
  25.9 0.1 sub.116
  26.4 0.9 select_reduce_fusion.7
  27.4 0.3 fusion.37
  27.7 0.5 select_reduce_fusion.9
  28.2 0.7 reshape.506.send_ref
  29.0 5.1 %pack.4.out_ref = bf16[144,128,128]{2,1,0:T(8,128)(2,1)} custom-call(s32[144]{0:T(256)} %reshape.506.send_ref, bf16[64,128,128]{2,1,0:T(8,128)(2,1)S(1)} %copy-done, bf16[64,128,128]{2,1,0:T(8,128)(2,1)} %collective-permute-done.b_ref.refs_1_), custom_call_target="tpu_custom_call" | custom-call | tf_op jit(solution)/shard_map/pack/pallas_call | solution.py:174
  34.1 102.7 %exchange.4.refs_4_ = bf16[144,128,128]{2,1,0:T(8,128)(2,1)} custom-call(bf16[144,128,128]{2,1,0:T(8,128)(2,1)} %pack.4.out_ref), custom_call_target="tpu_custom_call" | custom-call | bytes 150994944 | tf_op jit(solution)/shard_map/exchange/pallas_call | solution.py:272
  136.8 0.5 collective-permute-start.2
  137.4 0.2 reduce_sum.161
  137.6 0.7 fusion.38
  139.1 0.1 reshape.502
  139.2 0.7 reshape.507.send_ref
  139.9 0.4 compare_reduce_fusion
  140.3 0.3 convolution_convert_fusion.1
  140.7 0.4 fusion.36
  141.0 0.5 compare_select_fusion.12.pick_ref
  141.6 5.5 %pack.5.out_ref = bf16[144,128,128]{2,1,0:T(8,128)(2,1)} custom-call(s32[144]{0:T(256)} %reshape.507.send_ref, bf16[64,128,128]{2,1,0:T(8,128)(2,1)} %collective-permute-done.1.a_ref.refs_2_, bf16[64,128,128]{2,1,0:T(8,128)(2,1)} %collective-permute-done.2.b_ref.refs_3_), custom_call_target="tpu_custom_call" | custom-call | tf_op jit(solution)/shard_map/pack/pallas_call | solution.py:174
  147.1 67.7 %exchange.5.refs_5_ = bf16[144,128,128]{2,1,0:T(8,128)(2,1)} custom-call(bf16[144,128,128]{2,1,0:T(8,128)(2,1)} %pack.5.out_ref), custom_call_target="tpu_custom_call" | custom-call | bytes 150994944 | tf_op jit(solution)/shard_map/exchange/pallas_call | solution.py:272
  214.8 16.0 %tiles.7 = f32[2048,512]{1,0:T(8,128)} custom-call(s32[256]{0:T(256)} %compare_select_fusion.12.pick_ref, s32[64]{0:T(128)S(1)} %copy-done.1, bf16[64,128,128]{2,1,0:T(8,128)(2,1)S(1)} %copy-done, bf16[64,128,128]{2,1,0:T(8,128)(2,1)} %collective-permute-done.b_ref.refs_1_, bf16[64,128,128]{2,1,0:T(8,128)(2,1)} %collective-permute-done.1.a_ref.refs_2_, ...), custom_call_target="tpu_custom_call" | custom-call | tf_op jit(solution)/shard_map/tiles/pallas_call | solution.py:191
  (46 shorter events, 1.3 us)
Async XLA Ops:
  0.0 29.0 %copy-start = (bf16[64,128,128]{2,1,0:T(8,128)(2,1)S(1)}, bf16[64,128,128]{2,1,0:T(8,128)(2,1)}, u32[]{:S(2)}) copy-start(bf16[64,128,128]{2,1,0:T(8,128)(2,1)} %refs_0_.1) | copy-start | bytes 6291460
  18.2 118.5 %collective-permute-start.1 = (bf16[64,128,128]{2,1,0:T(8,128)(2,1)}, bf16[64,128,128]{2,1,0:T(8,128)(2,1)}, u32[]{:S(2)}, u32[]{:S(2)}) collective-permute-start(bf16[64,128,128]{2,1,0:T(8,128)(2,1)} %refs_0_.1), channel_id=1, source_target_pairs={{0,16},{1,17},{2,18},{3,19},{4,20},{5,21},{6,22},{7,23},{8,24},{9,... | collective-permute-start | bytes 6291464 | tf_op jit(solution)/shard_map/ppermute | solution.py:296
  19.0 9.9 %collective-permute-start = (bf16[64,128,128]{2,1,0:T(8,128)(2,1)}, bf16[64,128,128]{2,1,0:T(8,128)(2,1)}, u32[]{:S(2)}, u32[]{:S(2)}) collective-permute-start(bf16[64,128,128]{2,1,0:T(8,128)(2,1)} %refs_0_.1), channel_id=1, source_target_pairs={{0,1},{1,0},{2,3},{3,2},{4,5},{5,4},{6,7},{7,6},{8,9},{9,8},{10,11... | collective-permute-start | bytes 6291464 | tf_op jit(solution)/shard_map/ppermute | solution.py:297
  136.8 4.8 %collective-permute-start.2 = (bf16[64,128,128]{2,1,0:T(8,128)(2,1)}, bf16[64,128,128]{2,1,0:T(8,128)(2,1)}, u32[]{:S(2)}, u32[]{:S(2)}) collective-permute-start(bf16[64,128,128]{2,1,0:T(8,128)(2,1)} %collective-permute-done.1.a_ref.refs_2_), channel_id=1, source_target_pairs={{0,1},{1,0},{2,3},{3,2},{4,5},{5,4},{6,7},{7,6},{8,9},{9,8},{10,11... | collective-permute-start | bytes 6291464 | tf_op jit(solution)/shard_map/ppermute | solution.py:304
  147.1 67.7 %copy-start.1 = (s32[64]{0:T(128)S(1)}, s32[64]{0:T(128)}, u32[]{:S(2)}) copy-start(s32[64]{0:T(128)} %read_ref.1) | copy-start | bytes 772

commit v4 on v3

--- a/solution.py
+++ b/solution.py
@@ -58,7 +58,7 @@
     return jnp.max(jnp.where(c % families != d // CORES % families, demand, 0.0))
 
 
-def routes(table, blocks, lane):
+def routes(table, blocks):
     devices = lax.axis_size("dev")
     families = devices // FAMILY
     half_devices = devices // HALVES
@@ -96,24 +96,24 @@
     )
     f = iota(families, many, axis=0)
     part = i32(iota(families, many, axis=1) // (CORES * blocks) != half)
-    empty = many + HALVES * half_devices * lane
-
-    def send(turn, far):
-        spot = (turn * lane + iota(1, lane, 1, axis=1)) * CORES + core
+
+    def send(begin, lane, far):
+        spot = begin + iota(1, lane, 1, axis=1) * CORES + core
         chosen = jnp.where((x_half != half) == far, local % (CORES * blocks), 0)
         hit = (rank[:, None, :] == spot) & ((x_half != half) == far)
         return jnp.sum(jnp.where(hit, chosen[None, None, :], 0), axis=2).reshape(-1)
 
-    def pick(turn):
-        now = arrived - turn * lane * CORES
+    def pick(begin, lane, local):
+        empty = many + HALVES * half_devices * lane
+        now = arrived - begin
         there = (part * half_devices + f * CORES + now % CORES) * lane + now // CORES + many
         there = jnp.where((now >= 0) & (now < lane * CORES), there, empty)
-        place = jnp.where(f == family, jnp.where(turn == 0, local, empty)[None, :], there)
+        place = jnp.where(f == family, empty if local is None else local[None, :], there)
         place = place.reshape(families, HALVES, CORES * blocks).transpose(1, 0, 2).reshape(1, total)
         found = jnp.sum(jnp.where(match, place, 0), axis=1)
         return jnp.where(own > 0, found, empty)
 
-    return send, pick
+    return send, pick, local
 
 
 def fill(near, held, sems):
@@ -202,34 +202,47 @@
     )(pick, read_block, *near, *got)
 
 
-def everyone_kernel(devices, row_ref, out_ref, send_sems, recv_sems):
+def everyone_kernel(devices, group, row_ref, out_ref, send_sems, recv_sems):
     me = lax.axis_index("dev")
+    first = me // group * group
     out_ref[me] = row_ref[...]
-    copies = []
-    for k in range(1, devices):
-        copies.append(
-            pltpu.make_async_remote_copy(
-                src_ref=row_ref,
-                dst_ref=out_ref.at[me],
-                send_sem=send_sems.at[k],
-                recv_sem=recv_sems.at[k],
-                device_id=(lax.rem(me + k, devices),),
-                device_id_type=pl.DeviceIdType.MESH,
-            )
+
+    def spread(src, dst, to, k):
+        copy = pltpu.make_async_remote_copy(
+            src_ref=src,
+            dst_ref=dst,
+            send_sem=send_sems.at[k],
+            recv_sem=recv_sems.at[k],
+            device_id=(to,),
+            device_id_type=pl.DeviceIdType.MESH,
         )
-        copies[-1].start()
-    for copy in copies:
+        copy.start()
+        return copy
+
+    near = [
+        spread(row_ref, out_ref.at[me], first + (me - first + k) % group, k)
+        for k in range(1, group)
+    ]
+    for copy in near:
         copy.wait()
+    rows = out_ref.at[pl.ds(first, group)]
+    far = [
+        spread(rows, rows, (me + k * group) % devices, group + k)
+        for k in range(1, devices // group)
+    ]
+    for copy in far:
+        copy.wait()
 
 
 def gather_rows(row):
     devices = lax.axis_size("dev")
+    group = 1 << devices.bit_length() // 2
     return pl.pallas_call(
-        functools.partial(everyone_kernel, devices),
+        functools.partial(everyone_kernel, devices, group),
         out_shape=jax.ShapeDtypeStruct((devices,) + row.shape, row.dtype),
         in_specs=[VMEM],
         out_specs=VMEM,
-        scratch_shapes=[pltpu.SemaphoreType.DMA((devices,))] * 2,
+        scratch_shapes=[pltpu.SemaphoreType.DMA((group + devices // group,))] * 2,
         compiler_params=pltpu.CompilerParams(has_side_effects=True),
         name="gather_rows",
     )(row)
@@ -248,22 +261,36 @@
     me = lax.axis_index("dev")
     count = devices // HALVES
     spot = me % count
-    copies = []
-    for k in range(CORES, count):
+
+    def copy_of(k):
         to = flipped(spot, k)
-        copies.append(
-            pltpu.make_async_remote_copy(
-                src_ref=out_ref.at[pl.ds(to * lane, lane)],
-                dst_ref=got_ref.at[pl.ds(spot * lane, lane)],
-                send_sem=send_sems.at[k],
-                recv_sem=recv_sems.at[k],
-                device_id=(me - spot + to,),
-                device_id_type=pl.DeviceIdType.MESH,
-            )
+        return pltpu.make_async_remote_copy(
+            src_ref=out_ref.at[pl.ds(to * lane, lane)],
+            dst_ref=got_ref.at[pl.ds(spot * lane, lane)],
+            send_sem=send_sems.at[k],
+            recv_sem=recv_sems.at[k],
+            device_id=(me - spot + to,),
+            device_id_type=pl.DeviceIdType.MESH,
         )
-        copies[-1].start()
-    for copy in copies:
-        copy.wait()
+
+    chips = count // CORES
+    steps = []
+    for mask in range(chips - 1, chips // 2 - 1, -1):
+        for core in range(CORES):
+            masks = [m for m in (mask, chips - 1 - mask) if m]
+            steps.append([copy_of(m * CORES + core) for m in masks])
+    for i, step in enumerate(steps):
+        if i >= 2:
+            for copy in steps[i - 2]:
+                copy.wait_send()
+        for copy in step:
+            copy.start()
+    for step in steps[-2:]:
+        for copy in step:
+            copy.wait_send()
+    for step in steps:
+        for copy in step:
+            copy.wait_recv()
 
 
 def exchange(out, lane):
@@ -287,7 +314,8 @@
     devices = lax.axis_size("dev")
     blocks = occurrence.shape[0]
     slots = slot_order.shape[1]
-    lane = 2 * (2 * blocks // devices) + 1
+    lane = 2 * (2 * blocks // devices) + 2
+    spill = 2 * blocks // devices
     swap = [(d, d ^ 1) for d in range(devices)]
     across = [(d, (d + devices // HALVES) % devices) for d in range(devices)]
     row = jnp.stack([jnp.pad(block_owner[:, 0], (0, slots - blocks)), slot_order[0]])
@@ -297,22 +325,23 @@
     sibling = lax.ppermute(mine, "dev", swap)
     table = group_table(everyone[:, 0, :blocks], everyone[:, 1])
     most = i32(fullest_lane(table, blocks))
-    turns = (most + CORES * lane - 1) // (CORES * lane)
-    send, pick = routes(table, blocks, lane)
-    got = exchange(pack(send(0, False), (occurrence, sibling)), lane)
+    send, pick, local = routes(table, blocks)
+    begin = CORES * lane
+    got = exchange(pack(send(0, lane, False), (occurrence, sibling)), lane)
     far, got = lax.optimization_barrier((far, got))
     distant = (far, lax.ppermute(far, "dev", swap))
     near = (occurrence, sibling) + distant
-    also = exchange(pack(send(0, True), distant), lane)
-    first = tiles(pick(0), read_block, near, (got, also))
+    also = exchange(pack(send(0, lane, True), distant), lane)
+    first = tiles(pick(0, lane, local), read_block, near, (got, also))
 
     def more(carry):
-        turn, margin = carry
-        got = exchange(pack(send(turn, False), near[:CORES]), lane)
-        also = exchange(pack(send(turn, True), distant), lane)
-        return turn + 1, margin + tiles(pick(turn), read_block, near, (got, also))
-
-    return lax.while_loop(lambda carry: carry[0] < turns, more, (jnp.int32(1), first))[1]
+        begin, margin = carry
+        got = exchange(pack(send(begin, spill, False), near[:CORES]), spill)
+        also = exchange(pack(send(begin, spill, True), distant), spill)
+        added = tiles(pick(begin, spill, None), read_block, near, (got, also))
+        return begin + CORES * spill, margin + added
+
+    return lax.while_loop(lambda carry: carry[0] < most, more, (jnp.int32(begin), first))[1]
 
 
 def solution(mesh):

time: 231 us -> 238 us (1.030)
  Pallas kernels: 213 us -> 220 us
    pallas_call x2, Pallas kernels: 170 us -> 174 us  [exchange(): pl.pallas_call(functools.partial(exchange_kernel, devices, lane), out_sha...]
  transfers between devices with their start and end apart: 3 -> 3, of which waited for: 0 -> 0; matrix products, arithmetic and copies ran while one was open for 6% -> 6% of each run, Pallas kernels for 47% -> 48%
where the time goes in v4:
time: 238 us; the launch traced here: 237 us
  Pallas kernels  220 us (92%)
  other arithmetic  9.15 us (4%)
  local copies, waits for them, and re-layouts  5.01 us (2%)
    pallas_call x2, Pallas kernels, exchange(): pl.pallas_call(functools.partial(exchange_kernel, devices, lane), out_sha...  174 us
    pallas_call x1, Pallas kernels, gather_rows(): pl.pallas_call(functools.partial(everyone_kernel, devices, group), out_sh...  17.9 us
    pallas_call x1, Pallas kernels, tiles(): pl.pallas_call(tile_kernel, out_shape=jax.ShapeDtypeStruct((RB_DEV * rows...  16.3 us
    pallas_call x2, Pallas kernels, pack(): pl.pallas_call(pack_kernel, out_shape=jax.ShapeDtypeStruct((send.shape[0]...  11.1 us
  transfers between devices with their start and end apart: 3, of which 0 were waited for; matrix products, arithmetic and copies ran while one was open for 6% of the time, Pallas kernels for 48%

profile of v4, /device:TPU:0, one launch (start us, length us, event | category | flops | bytes accessed | tf_op | source)
XLA Modules:
  0.0 237.4 jit_solution(18250486466787952078)
XLA Ops:
  0.0 0.8 pad_bitcast_fusion
  0.8 1.2 pad_add_fusion.1.row_ref
  2.0 17.9 %gather_rows.1 = s32[32,2,128]{2,1,0:T(2,128)} custom-call(s32[2,128]{1,0:T(2,128)} %pad_add_fusion.1.row_ref), custom_call_target="tpu_custom_call" | custom-call | tf_op jit(solution)/shard_map/gather_rows/pallas_call | solution.py:240
  20.0 0.8 collective-permute-start.1
  20.8 0.8 slice.27
  21.6 0.8 slice.26
  22.4 0.9 convert_reduce_fusion
  23.4 0.7 select_reduce_fusion.8
  24.1 0.1 copy.25
  24.2 0.1 copy.26
  24.3 0.1 copy.23
  24.5 2.9 %select_reduce_fusion.3 = s32[4,32,32]{2,1,0:T(8,128)S(1)} fusion(s32[32,128]{1,0:T(8,128)S(1)} %copy.27, s32[4,32,32]{2,1,0:T(8,128)S(1)} %copy.24), kind=kLoop, calls=%fused_computation.70 | loop fusion | flops 1568768 | bytes 49152 | tf_op jit(solution)/shard_map/reduce_sum | solution.py:39
  27.5 0.1 gt.47
  27.6 0.1 sub.110
  28.2 0.9 select_reduce_fusion.7
  29.2 0.3 fusion.37
  29.5 0.5 select_reduce_fusion.9
  30.1 0.7 reshape.488.send_ref
  30.8 5.3 %pack.4.out_ref = bf16[160,128,128]{2,1,0:T(8,128)(2,1)} custom-call(s32[160]{0:T(256)} %reshape.488.send_ref, bf16[64,128,128]{2,1,0:T(8,128)(2,1)S(1)} %copy-done, bf16[64,128,128]{2,1,0:T(8,128)(2,1)} %collective-permute-done.b_ref.refs_1_), custom_call_target="tpu_custom_call" | custom-call | tf_op jit(solution)/shard_map/pack/pallas_call | solution.py:174
  36.1 108.1 %exchange.4.refs_4_ = bf16[160,128,128]{2,1,0:T(8,128)(2,1)} custom-call(bf16[160,128,128]{2,1,0:T(8,128)(2,1)} %pack.4.out_ref), custom_call_target="tpu_custom_call" | custom-call | bytes 167772160 | tf_op jit(solution)/shard_map/exchange/pallas_call | solution.py:299
  144.2 0.5 collective-permute-start.2
  144.7 0.1 reshape.484
  144.9 0.7 reshape.489.send_ref
  145.7 0.2 reduce_sum.161
  145.9 0.8 fusion.38
  147.4 0.4 compare_reduce_fusion
  147.8 0.3 convolution_convert_fusion.1
  148.1 0.4 fusion.36
  148.5 0.6 compare_select_fusion.12.pick_ref
  149.1 5.8 %pack.5.out_ref = bf16[160,128,128]{2,1,0:T(8,128)(2,1)} custom-call(s32[160]{0:T(256)} %reshape.489.send_ref, bf16[64,128,128]{2,1,0:T(8,128)(2,1)} %collective-permute-done.1.a_ref.refs_2_, bf16[64,128,128]{2,1,0:T(8,128)(2,1)} %collective-permute-done.2.b_ref.refs_3_), custom_call_target="tpu_custom_call" | custom-call | tf_op jit(solution)/shard_map/pack/pallas_call | solution.py:174
  154.9 66.1 %exchange.5.refs_5_ = bf16[160,128,128]{2,1,0:T(8,128)(2,1)} custom-call(bf16[160,128,128]{2,1,0:T(8,128)(2,1)} %pack.5.out_ref), custom_call_target="tpu_custom_call" | custom-call | bytes 167772160 | tf_op jit(solution)/shard_map/exchange/pallas_call | solution.py:299
  221.1 16.3 %tiles.7 = f32[2048,512]{1,0:T(8,128)} custom-call(s32[256]{0:T(256)} %compare_select_fusion.12.pick_ref, s32[64]{0:T(128)S(1)} %copy-done.1, bf16[64,128,128]{2,1,0:T(8,128)(2,1)S(1)} %copy-done, bf16[64,128,128]{2,1,0:T(8,128)(2,1)} %collective-permute-done.b_ref.refs_1_, bf16[64,128,128]{2,1,0:T(8,128)(2,1)} %collective-permute-done.1.a_ref.refs_2_, ...), custom_call_target="tpu_custom_call" | custom-call | tf_op jit(solution)/shard_map/tiles/pallas_call | solution.py:191
  (46 shorter events, 1.3 us)
Async XLA Ops:
  0.0 30.8 %copy-start = (bf16[64,128,128]{2,1,0:T(8,128)(2,1)S(1)}, bf16[64,128,128]{2,1,0:T(8,128)(2,1)}, u32[]{:S(2)}) copy-start(bf16[64,128,128]{2,1,0:T(8,128)(2,1)} %refs_0_.1) | copy-start | bytes 6291460
  20.0 124.2 %collective-permute-start.1 = (bf16[64,128,128]{2,1,0:T(8,128)(2,1)}, bf16[64,128,128]{2,1,0:T(8,128)(2,1)}, u32[]{:S(2)}, u32[]{:S(2)}) collective-permute-start(bf16[64,128,128]{2,1,0:T(8,128)(2,1)} %refs_0_.1), channel_id=1, source_target_pairs={{0,16},{1,17},{2,18},{3,19},{4,20},{5,21},{6,22},{7,23},{8,24},{9,... | collective-permute-start | bytes 6291464 | tf_op jit(solution)/shard_map/ppermute | solution.py:324
  20.8 10.0 %collective-permute-start = (bf16[64,128,128]{2,1,0:T(8,128)(2,1)}, bf16[64,128,128]{2,1,0:T(8,128)(2,1)}, u32[]{:S(2)}, u32[]{:S(2)}) collective-permute-start(bf16[64,128,128]{2,1,0:T(8,128)(2,1)} %refs_0_.1), channel_id=1, source_target_pairs={{0,1},{1,0},{2,3},{3,2},{4,5},{5,4},{6,7},{7,6},{8,9},{9,8},{10,11... | collective-permute-start | bytes 6291464 | tf_op jit(solution)/shard_map/ppermute | solution.py:325
  144.2 4.9 %collective-permute-start.2 = (bf16[64,128,128]{2,1,0:T(8,128)(2,1)}, bf16[64,128,128]{2,1,0:T(8,128)(2,1)}, u32[]{:S(2)}, u32[]{:S(2)}) collective-permute-start(bf16[64,128,128]{2,1,0:T(8,128)(2,1)} %collective-permute-done.1.a_ref.refs_2_), channel_id=1, source_target_pairs={{0,1},{1,0},{2,3},{3,2},{4,5},{5,4},{6,7},{7,6},{8,9},{9,8},{10,11... | collective-permute-start | bytes 6291464 | tf_op jit(solution)/shard_map/ppermute | solution.py:332
  154.9 66.1 %copy-start.1 = (s32[64]{0:T(128)S(1)}, s32[64]{0:T(128)}, u32[]{:S(2)}) copy-start(s32[64]{0:T(128)} %read_ref.1) | copy-start | bytes 772

commit v5 on v4

--- a/solution.py
+++ b/solution.py
@@ -314,7 +314,7 @@
     devices = lax.axis_size("dev")
     blocks = occurrence.shape[0]
     slots = slot_order.shape[1]
-    lane = 2 * (2 * blocks // devices) + 2
+    lane = 2 * (2 * blocks // devices) + 1
     spill = 2 * blocks // devices
     swap = [(d, d ^ 1) for d in range(devices)]
     across = [(d, (d + devices // HALVES) % devices) for d in range(devices)]

time: 238 us -> 223 us (0.937)
  Pallas kernels: 220 us -> 205 us
    pallas_call x2, Pallas kernels: 174 us -> 160 us  [exchange(): pl.pallas_call(functools.partial(exchange_kernel, devices, lane), out_sha...]
where the time goes in v5:
time: 223 us
  Pallas kernels  205 us (92%)
  other arithmetic  9.12 us (4%)
  local copies, waits for them, and re-layouts  5.01 us (2%)
    pallas_call x2, Pallas kernels, exchange(): pl.pallas_call(functools.partial(exchange_kernel, devices, lane), out_sha...  160 us
    pallas_call x1, Pallas kernels, gather_rows(): pl.pallas_call(functools.partial(everyone_kernel, devices, group), out_sh...  17.9 us
    pallas_call x1, Pallas kernels, tiles(): pl.pallas_call(tile_kernel, out_shape=jax.ShapeDtypeStruct((RB_DEV * rows...  16 us
    pallas_call x2, Pallas kernels, pack(): pl.pallas_call(pack_kernel, out_shape=jax.ShapeDtypeStruct((send.shape[0]...  10.7 us
  transfers between devices with their start and end apart: 3, of which 0 were waited for; matrix products, arithmetic and copies ran while one was open for 6% of the time, Pallas kernels for 48%

profile of v5, /device:TPU:0, one launch (start us, length us, event | category | flops | bytes accessed | tf_op | source)
XLA Modules:
  0.0 222.7 jit_solution(10431108965221943658)
XLA Ops:
  0.0 0.8 pad_bitcast_fusion
  0.8 1.2 pad_add_fusion.1.row_ref
  2.0 17.9 %gather_rows.1 = s32[32,2,128]{2,1,0:T(2,128)} custom-call(s32[2,128]{1,0:T(2,128)} %pad_add_fusion.1.row_ref), custom_call_target="tpu_custom_call" | custom-call | tf_op jit(solution)/shard_map/gather_rows/pallas_call | solution.py:240
  20.0 0.8 collective-permute-start.1
  20.8 0.8 slice.27
  21.6 0.8 slice.26
  22.4 0.9 convert_reduce_fusion
  23.4 0.7 select_reduce_fusion.8
  24.1 0.1 copy.25
  24.2 0.1 copy.26
  24.3 0.1 copy.23
  24.5 2.9 %select_reduce_fusion.3 = s32[4,32,32]{2,1,0:T(8,128)S(1)} fusion(s32[32,128]{1,0:T(8,128)S(1)} %copy.27, s32[4,32,32]{2,1,0:T(8,128)S(1)} %copy.24), kind=kLoop, calls=%fused_computation.70 | loop fusion | flops 1568768 | bytes 49152 | tf_op jit(solution)/shard_map/reduce_sum | solution.py:39
  27.5 0.1 gt.47
  27.6 0.1 sub.110
  28.2 0.9 select_reduce_fusion.7
  29.2 0.3 fusion.37
  29.5 0.5 select_reduce_fusion.9
  30.0 0.7 reshape.488.send_ref
  30.7 5.1 %pack.4.out_ref = bf16[144,128,128]{2,1,0:T(8,128)(2,1)} custom-call(s32[144]{0:T(256)} %reshape.488.send_ref, bf16[64,128,128]{2,1,0:T(8,128)(2,1)S(1)} %copy-done, bf16[64,128,128]{2,1,0:T(8,128)(2,1)} %collective-permute-done.b_ref.refs_1_), custom_call_target="tpu_custom_call" | custom-call | tf_op jit(solution)/shard_map/pack/pallas_call | solution.py:174
  35.8 101.6 %exchange.4.refs_4_ = bf16[144,128,128]{2,1,0:T(8,128)(2,1)} custom-call(bf16[144,128,128]{2,1,0:T(8,128)(2,1)} %pack.4.out_ref), custom_call_target="tpu_custom_call" | custom-call | bytes 150994944 | tf_op jit(solution)/shard_map/exchange/pallas_call | solution.py:299
  137.4 0.5 collective-permute-start.2
  138.0 0.1 reshape.484
  138.1 0.7 reshape.489.send_ref
  138.9 0.2 reduce_sum.161
  139.1 0.8 fusion.38
  140.7 0.4 compare_reduce_fusion
  141.1 0.3 convolution_convert_fusion.1
  141.4 0.4 fusion.36
  141.8 0.6 compare_select_fusion.12.pick_ref
  142.4 5.6 %pack.5.out_ref = bf16[144,128,128]{2,1,0:T(8,128)(2,1)} custom-call(s32[144]{0:T(256)} %reshape.489.send_ref, bf16[64,128,128]{2,1,0:T(8,128)(2,1)} %collective-permute-done.1.a_ref.refs_2_, bf16[64,128,128]{2,1,0:T(8,128)(2,1)} %collective-permute-done.2.b_ref.refs_3_), custom_call_target="tpu_custom_call" | custom-call | tf_op jit(solution)/shard_map/pack/pallas_call | solution.py:174
  148.1 58.6 %exchange.5.refs_5_ = bf16[144,128,128]{2,1,0:T(8,128)(2,1)} custom-call(bf16[144,128,128]{2,1,0:T(8,128)(2,1)} %pack.5.out_ref), custom_call_target="tpu_custom_call" | custom-call | bytes 150994944 | tf_op jit(solution)/shard_map/exchange/pallas_call | solution.py:299
  206.7 16.0 %tiles.7 = f32[2048,512]{1,0:T(8,128)} custom-call(s32[256]{0:T(256)} %compare_select_fusion.12.pick_ref, s32[64]{0:T(128)S(1)} %copy-done.1, bf16[64,128,128]{2,1,0:T(8,128)(2,1)S(1)} %copy-done, bf16[64,128,128]{2,1,0:T(8,128)(2,1)} %collective-permute-done.b_ref.refs_1_, bf16[64,128,128]{2,1,0:T(8,128)(2,1)} %collective-permute-done.1.a_ref.refs_2_, ...), custom_call_target="tpu_custom_call" | custom-call | tf_op jit(solution)/shard_map/tiles/pallas_call | solution.py:191
  (46 shorter events, 1.3 us)
Async XLA Ops:
  0.0 30.7 %copy-start = (bf16[64,128,128]{2,1,0:T(8,128)(2,1)S(1)}, bf16[64,128,128]{2,1,0:T(8,128)(2,1)}, u32[]{:S(2)}) copy-start(bf16[64,128,128]{2,1,0:T(8,128)(2,1)} %refs_0_.1) | copy-start | bytes 6291460
  20.0 117.4 %collective-permute-start.1 = (bf16[64,128,128]{2,1,0:T(8,128)(2,1)}, bf16[64,128,128]{2,1,0:T(8,128)(2,1)}, u32[]{:S(2)}, u32[]{:S(2)}) collective-permute-start(bf16[64,128,128]{2,1,0:T(8,128)(2,1)} %refs_0_.1), channel_id=1, source_target_pairs={{0,16},{1,17},{2,18},{3,19},{4,20},{5,21},{6,22},{7,23},{8,24},{9,... | collective-permute-start | bytes 6291464 | tf_op jit(solution)/shard_map/ppermute | solution.py:324
  20.8 9.9 %collective-permute-start = (bf16[64,128,128]{2,1,0:T(8,128)(2,1)}, bf16[64,128,128]{2,1,0:T(8,128)(2,1)}, u32[]{:S(2)}, u32[]{:S(2)}) collective-permute-start(bf16[64,128,128]{2,1,0:T(8,128)(2,1)} %refs_0_.1), channel_id=1, source_target_pairs={{0,1},{1,0},{2,3},{3,2},{4,5},{5,4},{6,7},{7,6},{8,9},{9,8},{10,11... | collective-permute-start | bytes 6291464 | tf_op jit(solution)/shard_map/ppermute | solution.py:325
  137.4 5.0 %collective-permute-start.2 = (bf16[64,128,128]{2,1,0:T(8,128)(2,1)}, bf16[64,128,128]{2,1,0:T(8,128)(2,1)}, u32[]{:S(2)}, u32[]{:S(2)}) collective-permute-start(bf16[64,128,128]{2,1,0:T(8,128)(2,1)} %collective-permute-done.1.a_ref.refs_2_), channel_id=1, source_target_pairs={{0,1},{1,0},{2,3},{3,2},{4,5},{5,4},{6,7},{7,6},{8,9},{9,8},{10,11... | collective-permute-start | bytes 6291464 | tf_op jit(solution)/shard_map/ppermute | solution.py:332
  148.0 58.7 %copy-start.1 = (s32[64]{0:T(128)S(1)}, s32[64]{0:T(128)}, u32[]{:S(2)}) copy-start(s32[64]{0:T(128)} %read_ref.1) | copy-start | bytes 772
